TPU v7x, 128 devices: a whole 4x4x4 slice. The times are simulated.
128 devices in a mesh: seq: 16 (over z, x), tp: 8 (over y, core).
Axes of the slice: x: 4, y: 4, z: 4, core: 2. Of those that a mesh axis runs over, the one named last changes fastest.
Arguments:
- inner_x: bfloat16 [8192, 5120], P('seq', 'tp'), may hold values from -6 to 6
- gate_z: bfloat16 [8192, 5120], P('seq', 'tp'), may hold values from -6 to 6
- proj_bc: bfloat16 [8192, 256], P('seq'), may hold values from -6 to 6
- dt_raw: bfloat16 [8192, 80], P('seq', 'tp'), may hold values from -6 to 10
- a_log: float32 [80], P('tp'), may hold values from -12 to 0
- dt_bias: float32 [80], P('tp'), may hold values from -4 to -2
- d_skip: float32 [80], P('tp'), may hold values from 0.5 to 1.5
- conv_x: float32 [4, 5120], P(None, 'tp'), may hold values from -3 to 3
- bias_x: float32 [5120], P('tp'), may hold values from -3 to 3
- conv_bc: float32 [4, 256], replicated, may hold values from -3 to 3
- bias_bc: float32 [256], replicated, may hold values from -3 to 3
- norm_gain: float32 [5120], P('tp'), may hold values from 0.5 to 1.5
- w_out: bfloat16 [5120, 2560], P('tp', 'seq'), may hold values from -0.078125 to 0.078125
- d_out: bfloat16 [8192, 2560], P('seq', 'tp'), may hold values from -6 to 6
Outputs:
- output: bfloat16 [8192, 2560], P('seq', 'tp')
- grad_x: float32 [8192, 5120], P('seq', 'tp')
- grad_z: float32 [8192, 5120], P('seq', 'tp')
- grad_bc: float32 [8192, 256], P('seq')
- grad_dt: float32 [8192, 80], P('seq', 'tp')
- grad_w: float32 [5120, 2560], P('tp', 'seq')
All inputs are finite; a program needn't handle non-finite values.
Results may differ from a plain program's by a relative error of at most 0.013.
Values may be sent and summed in bfloat16 or wider, within the bound.
A program may use at most 192 MiB of HBM per device.

v0:
```python
import functools

import jax
import jax.numpy as jnp
from jax import lax
from jax.experimental import pallas as pl
from jax.experimental.pallas import tpu as pltpu
from jax.sharding import PartitionSpec as P

MESH = pl.DeviceIdType.MESH
F32 = jnp.float32
BF16 = jnp.bfloat16
HIGH = lax.Precision.HIGHEST
EPSILON = 1e-05
NN = ((1,), (0,))
NT = ((1,), (1,))
Q = 128
PAIR = 128
HEAD = 64
LANES = 128


def mm(a, b, dims=NN):
    return lax.dot_general(a.astype(BF16), b.astype(BF16), (dims, ((), ())), preferred_element_type=F32)


def mmh(a, b, dims=NN):
    return lax.dot_general(
        a.astype(F32), b.astype(F32), (dims, ((), ())), precision=HIGH, preferred_element_type=F32
    )


def halves(v):
    high = v.astype(BF16)
    return high, (v - high.astype(F32)).astype(BF16)


def mm3(a, b, dims=NN):
    a0, a1 = halves(a)
    b0, b1 = halves(b)
    return mm(a0, b0, dims) + (mm(a1, b0, dims) + mm(a0, b1, dims))


def iota(shape, dim):
    return lax.broadcasted_iota(jnp.int32, shape, dim)


def sigmoid(v):
    return 1.0 / (1.0 + jnp.exp(-v))


def softplus(v):
    return jnp.maximum(v, 0.0) + jnp.log1p(jnp.exp(-jnp.abs(v)))


def pair_stack(v):
    lane = iota(v.shape, 1)
    return jnp.concatenate(
        [jnp.where(lane < HEAD, v, 0.0), jnp.where(lane >= HEAD, v, 0.0)], axis=0
    )


def kernel(
    sizes,
    ix,
    gz,
    bc,
    raw,
    wt,
    dt,
    cw,
    bx,
    cwb,
    bb,
    gain,
    al,
    db,
    ds,
    alc,
    dbc,
    o_out,
    o_gx,
    o_gz,
    o_gbc,
    o_gdt,
    o_gw,
    wfull,
    dfull,
    hx,
    hb,
    dsend,
    dbuf,
    st,
    lx,
    lt,
    u,
    x,
    ub,
    bcv,
    fr,
    sst,
    cf,
    y,
    gated,
    gn,
    gm,
    nb,
    dxs,
    dus,
    dub,
    rcur,
    se,
    sr,
    en,
    sin,
    re,
    rr,
    ren,
    rin,
    ts,
    tr,
    pb,
    pr,
    gb,
    gr,
    qs,
    qr,
    qa,
    arow,
    acol,
    dga,
    sm_h,
    sm_d,
    sm_w,
    sm_g,
    sm_s,
    sm_b,
    sm_r,
    sm_q,
    sm_t,
    sm_o,
    sm_v,
    sm_p,
    sm_a,
):
    n_seq, n_tp, inner = sizes
    rows, ch = ix.shape
    nc = rows // Q
    heads = ch // HEAD
    pairs = ch // PAIR
    ns = bc.shape[1] // 2
    me, my = lax.axis_index("seq"), lax.axis_index("tp")
    wrows = wt.shape[0]
    drows = dt.shape[0]
    nrow = ns // n_seq

    scope = []

    def phase(name):
        if scope:
            scope.pop().__exit__(None, None, None)
        if name:
            scope.append(jax.named_scope(name))
            scope[0].__enter__()

    def seq_peer(k):
        return lax.rem(me + k, n_seq)

    def tp_peer(k):
        return lax.rem(my + k, n_tp)

    phase("barrier")
    barrier = pltpu.get_barrier_semaphore()
    for k in range(1, n_seq):
        pl.semaphore_signal(barrier, inc=1, device_id={"seq": seq_peer(k)}, device_id_type=MESH)
    for k in range(1, n_tp):
        pl.semaphore_signal(barrier, inc=1, device_id={"tp": tp_peer(k)}, device_id_type=MESH)
    pl.semaphore_wait(barrier, n_seq + n_tp - 2)

    def remote(src, dst, sems, k, axis, peer):
        return pltpu.make_async_remote_copy(
            src_ref=src,
            dst_ref=dst,
            send_sem=sems.at[0, k],
            recv_sem=sems.at[1, k],
            device_id={axis: peer},
            device_id_type=MESH,
        )

    phase("start")
    nxt, prv = seq_peer(1), seq_peer(n_seq - 1)
    halo_x = remote(ix.at[pl.ds(rows - 16, 16)], hx, sm_h, 0, "seq", nxt)
    halo_b = remote(bc.at[pl.ds(rows - 16, 16)], hb, sm_h, 1, "seq", nxt)
    halo_x.start()
    halo_b.start()

    def w_copy(k):
        return remote(wt, wfull.at[pl.ds(me * wrows, wrows)], sm_w, k, "seq", seq_peer(k))

    def d_copy(k):
        return remote(dt, dfull.at[pl.ds(my * drows, drows)], sm_g, k, "tp", tp_peer(k))

    for k in range(1, n_tp):
        d_copy(k).start()
    own_w = pltpu.make_async_copy(wt, wfull.at[pl.ds(me * wrows, wrows)], sm_w.at[0, 0])
    own_d = pltpu.make_async_copy(dt, dfull.at[pl.ds(my * drows, drows)], sm_g.at[0, 0])
    own_w.start()
    own_d.start()

    phase("steps")
    spread = (iota((LANES, ch), 1) // HEAD == iota((LANES, ch), 0)).astype(F32)
    spread_h = spread[:heads]
    negexp = -jnp.exp(al[...])
    neg_x = mmh(jnp.broadcast_to(negexp, (8, heads)), spread_h)[0:1]
    dtb_x = mmh(jnp.broadcast_to(db[...], (8, heads)), spread_h)[0:1]
    skip_x = mmh(jnp.broadcast_to(ds[...], (8, heads)), spread_h)[0:1]
    tri = (iota((Q, Q), 0) >= iota((Q, Q), 1)).astype(F32)
    tri_u = (iota((Q, Q), 0) <= iota((Q, Q), 1)).astype(F32)
    strict = (iota((Q, Q), 0) > iota((Q, Q), 1)).astype(F32)

    ident = (iota((16, heads), 0) == iota((16, heads), 1)).astype(F32)

    def steps(c, total):
        sl = pl.ds(pl.multiple_of(c * Q, Q), Q)
        r = raw[sl, :]
        s = softplus(mm(r, spread_h) + dtb_x)
        ld = s * neg_x
        cum = mmh(tri, ld)
        st[sl, :] = s
        lx[sl, :] = cum
        s_t = softplus(mm(ident, r, NT) + dbc[...])
        lt[c] = mmh(s_t * -jnp.exp(alc[...]), tri_u)
        return total + cum[Q - 1 : Q, :]

    total = lax.fori_loop(0, nc, steps, jnp.zeros((1, ch), F32))
    pick = (iota((ch, LANES), 0) == iota((ch, LANES), 1) * HEAD).astype(F32)
    dsend[...] = mmh(jnp.broadcast_to(total, (8, ch)), pick)

    def t_copy(k):
        return remote(dsend, dbuf.at[me], sm_d, k, "seq", seq_peer(k))

    dbuf[me] = dsend[...]
    for k in range(1, n_seq):
        t_copy(k).start()

    phase("wait_halo")
    halo_x.wait_recv()
    halo_b.wait_recv()

    phase("convs")
    def conv_of(ref, halo, weights, bias, c):
        base = pl.multiple_of(c * Q, Q)
        own = ref[pl.ds(base, Q), :].astype(F32)
        before = pl.multiple_of(jnp.maximum(c * Q - 16, 0), 16)
        prev = ref[pl.ds(before, 16), :].astype(F32)
        edge = jnp.where(me > 0, halo[...].astype(F32), 0.0)
        head = jnp.where(c > 0, prev, edge)[8:16]
        ext = jnp.concatenate([head, own], axis=0)
        acc = bias[...] + weights[3:4, :] * own
        for k in range(3):
            acc = acc + weights[k : k + 1, :] * pltpu.roll(ext, Q + 8 - (5 + k), 0)[:Q]
        return acc

    def convs(c, carry):
        sl = pl.ds(pl.multiple_of(c * Q, Q), Q)
        vb = conv_of(bc, hb, cwb, bb, c)
        ub[sl, :] = vb
        pbc = vb * sigmoid(vb)
        bcv[sl, :] = pbc
        vx = conv_of(ix, hx, cw, bx, c)
        u[sl, :] = vx
        xv = vx * sigmoid(vx)
        x[sl, :] = xv
        cum = lx[sl, :]
        to_end = jnp.exp(cum[Q - 1 : Q, :] - cum)
        b_t = jnp.transpose(pbc[:, :ns])
        fresh = mm3(b_t, xv * st[sl, :] * to_end)
        fr[c] = fresh
        return jnp.exp(cum[Q - 1 : Q, :]) * carry + fresh

    end = lax.fori_loop(0, nc, convs, jnp.zeros((ns, ch), F32))
    se[...] = end.reshape(n_seq, nrow, ch)

    phase("send_s")
    def s_copy(k):
        return remote(se.at[seq_peer(k)], sr.at[me], sm_s, k, "seq", seq_peer(k))

    def sb_copy(k):
        return remote(en.at[seq_peer(k)], sin.at[me], sm_b, k, "seq", seq_peer(k))

    for k in range(1, n_seq):
        s_copy(k).start()
    sr[me] = se[me]
    for k in range(1, n_seq):
        w_copy(k).start()

    upper = iota((Q, Q), 0) >= iota((Q, Q), 1)
    lower = iota((Q, Q), 0) <= iota((Q, Q), 1)

    phase("inside")
    def inside(c, carry):
        sl = pl.ds(pl.multiple_of(c * Q, Q), Q)
        scores = mm3(bcv[sl, ns:], bcv[sl, :ns], NT)
        for p in range(pairs):
            ps = slice(p * PAIR, (p + 1) * PAIR)
            both = []
            for h in (2 * p, 2 * p + 1):
                diff = lx[sl, h * HEAD : h * HEAD + 1] - lt[c, h : h + 1, :]
                decay = jnp.exp(jnp.where(upper, diff, -1e30))
                both.append(decay * scores)
            y[sl, ps] = mm3(jnp.concatenate(both, axis=1), pair_stack(x[sl, ps] * st[sl, ps]))
        return carry

    lax.fori_loop(0, nc, inside, 0)

    phase("wait_s")
    for k in range(1, n_seq):
        t_copy(k).wait_recv()
    for k in range(1, n_seq):
        s_copy(k).wait_recv()
    phase("scan")
    spread_d = mmh(dbuf[...].reshape(n_seq * 8, LANES), spread)

    acc = jnp.zeros((nrow, ch), F32)
    for j in range(n_seq):
        en[j] = acc
        acc = jnp.exp(spread_d[8 * j : 8 * j + 1]) * acc + sr[j]
    for k in range(1, n_seq):
        sb_copy(k).start()
    sin[me] = en[me]

    phase("wait_wd")
    own_d.wait()
    for k in range(1, n_tp):
        d_copy(k).wait_recv()
    own_w.wait()
    for k in range(1, n_seq):
        w_copy(k).wait_recv()

    phase("gn")
    width = wrows * n_seq
    kb = 512

    def gn_block(b, carry):
        kk = pl.ds(pl.multiple_of(b * kb, kb), kb)
        part = mm(jnp.transpose(dfull[kk, :]), wfull[kk, :])

        @pl.when(b == 0)
        def _():
            gn[...] = part

        @pl.when(b > 0)
        def _():
            gn[...] += part

        return carry

    lax.fori_loop(0, width // kb, gn_block, 0)

    phase("wait_sb")
    for k in range(1, n_seq):
        sb_copy(k).wait_recv()

    phase("combine")
    lane = iota((Q, LANES), 1)

    def combine(c, state):
        sl = pl.ds(pl.multiple_of(c * Q, Q), Q)
        sst[c] = state
        cum = lx[sl, :]
        mixed = y[sl, :] + jnp.exp(cum) * mm3(bcv[sl, ns:], state) + skip_x * x[sl, :]
        y[sl, :] = mixed
        zv = gz[sl, :].astype(F32)
        gv = mixed * zv * sigmoid(zv)
        gated[sl, :] = gv
        sq = jnp.sum(gv * gv, axis=1, keepdims=True)
        ip = jnp.sum(gn[sl, :] * gain[...] * gv, axis=1, keepdims=True)
        both = jnp.where(lane == 0, sq, jnp.where(lane == 1, ip, 0.0))
        ts[:, pl.ds(pl.multiple_of(c * Q, Q), Q)] = jnp.transpose(both)[:8]
        return jnp.exp(cum[Q - 1 : Q, :]) * state + fr[c]

    lax.fori_loop(0, nc, combine, sin[...].reshape(ns, ch))

    phase("wait_t")
    def r_copy(k):
        return remote(ts, tr.at[my], sm_t, k, "tp", tp_peer(k))

    for k in range(1, n_tp):
        r_copy(k).start()
    tr[my] = ts[...]
    for k in range(1, n_tp):
        r_copy(k).wait_recv()
    phase("norm")
    tsum = tr[0]
    for j in range(1, n_tp):
        tsum = tsum + tr[j]
    gn_pad = jnp.concatenate([tsum, jnp.zeros((Q - 8, rows), F32)], axis=0)
    ts2 = [jnp.transpose(gn_pad[:, c * Q : (c + 1) * Q]) for c in range(nc)]

    for c in range(nc):
        sl = pl.ds(c * Q, Q)
        inv = lax.rsqrt(ts2[c][:, 0:1] / inner + EPSILON)
        coef = inv * inv * inv * ts2[c][:, 1:2] / inner
        gv = gated[sl, :]
        nb[sl, :] = (gv * inv * gain[...]).astype(BF16)
        gg = inv * (gn[sl, :] * gain[...]) - gv * coef
        zv = gz[sl, :].astype(F32)
        sg = sigmoid(zv)
        o_gz[sl, :] = gg * y[sl, :] * sg * (1.0 + zv * (1.0 - sg))
        gmv = gg * zv * sg
        gm[sl, :] = gmv
        c_t = jnp.transpose(bcv[sl, ns:])
        cf[c] = mm3(c_t, gmv * jnp.exp(lx[sl, :]))

    racc = cf[nc - 1]
    for c in reversed(range(nc - 1)):
        racc = cf[c] + jnp.exp(lx[pl.ds(c * Q + Q - 1, 1), :]) * racc
    re[...] = racc.reshape(n_seq, nrow, ch)

    phase("send_v")
    def v_copy(k):
        return remote(re.at[seq_peer(k)], rr.at[me], sm_r, k, "seq", seq_peer(k))

    def vb_copy(k):
        return remote(ren.at[seq_peer(k)], rin.at[me], sm_q, k, "seq", seq_peer(k))

    for k in range(1, n_seq):
        v_copy(k).start()
    rr[me] = re[me]

    phase("outmm")
    def o_copy(k):
        return remote(pb.at[tp_peer(k)], pr.at[my], sm_o, k, "tp", tp_peer(k))

    for k in range(1, n_tp):
        d = tp_peer(k)
        block = wfull[pl.ds(pl.multiple_of(d * drows, drows), drows), :]
        pb[d] = mm(block, nb[...], NT).astype(BF16)
        o_copy(k).start()
    block = wfull[pl.ds(pl.multiple_of(my * drows, drows), drows), :]
    pr[my] = mm(block, nb[...], NT).astype(BF16)

    phase("wait_v")
    for k in range(1, n_seq):
        v_copy(k).wait_recv()
    acc = jnp.zeros((nrow, ch), F32)
    for j in reversed(range(n_seq)):
        ren[j] = acc
        acc = jnp.exp(spread_d[8 * j : 8 * j + 1]) * acc + rr[j]
    for k in range(1, n_seq):
        vb_copy(k).start()
    rin[me] = ren[me]

    phase("gradw")
    def g_copy(k):
        return remote(gb.at[seq_peer(k)], gr.at[me], sm_v, k, "seq", seq_peer(k))

    for k in range(1, n_seq):
        d = seq_peer(k)
        block = dfull[pl.ds(pl.multiple_of(d * wrows, wrows), wrows), :]
        gb[d] = mm(block, nb[...]).astype(BF16)
        g_copy(k).start()
    block = dfull[pl.ds(pl.multiple_of(me * wrows, wrows), wrows), :]
    gr[me] = mm(block, nb[...]).astype(BF16)

    phase("wait_vb")
    for k in range(1, n_seq):
        vb_copy(k).wait_recv()
    phase("back")
    rcur[...] = rin[...].reshape(ns, ch)

    to_head = (iota((ch, LANES), 0) // HEAD == iota((ch, LANES), 1)).astype(F32)
    neg_c = jnp.concatenate([negexp, jnp.zeros((1, LANES - heads), F32)], axis=1)
    blk = rows // n_tp

    def back(i, carry):
        c = nc - 1 - i
        sl = pl.ds(pl.multiple_of(c * Q, Q), Q)
        bmap, cmap = bcv[sl, :ns], bcv[sl, ns:]
        scores = mm3(cmap, bmap, NT)
        scores_t = mm3(bmap, cmap, NT)
        arow[...] = jnp.zeros((Q, LANES), F32)
        acol[...] = jnp.zeros((LANES, Q), F32)
        dga[...] = jnp.zeros((Q, Q), F32)
        for p in range(pairs):
            ps = slice(p * PAIR, (p + 1) * PAIR)
            g2 = gm[sl, ps]
            cross = mm3(g2, pair_stack(x[sl, ps] * st[sl, ps]), NT)
            both = []
            for i_h, h in enumerate((2 * p, 2 * p + 1)):
                diff = lx[sl, h * HEAD : h * HEAD + 1] - lt[c, h : h + 1, :]
                weighted = jnp.exp(jnp.where(upper, diff, -1e30)) * cross[:, i_h * Q : (i_h + 1) * Q]
                dga[...] += weighted
                term = weighted * scores
                arow[...] += jnp.where(lane == h, jnp.sum(term, axis=1, keepdims=True), 0.0)
                acol[h : h + 1, :] = jnp.sum(term, axis=0, keepdims=True)
                diff_t = lt[c, h : h + 1, :] - lx[sl, h * HEAD : h * HEAD + 1]
                decay_t = jnp.exp(jnp.where(lower, diff_t, -1e30))
                both.append((decay_t * scores_t).astype(BF16))
            dxs[:, ps] = mm(jnp.concatenate(both, axis=1), pair_stack(g2))
        cum = lx[sl, :]
        last = cum[Q - 1 : Q, :]
        grown = jnp.exp(cum)
        to_end = jnp.exp(last - cum)
        rv = rcur[...]
        sv = sst[c]
        gv = gm[sl, :]
        xv = x[sl, :]
        sx = st[sl, :]
        gg = gv * grown
        d_in = mm(bmap, rv) * to_end
        dxt = dxs[...] + d_in
        xt = xv * sx
        per_head = mmh(
            jnp.concatenate([gg * mm(cmap, sv), xt * d_in, xv * dxt], axis=0), to_head
        )
        fixed = mmh(
            jnp.broadcast_to(jnp.sum(rv * sv, axis=0, keepdims=True) * jnp.exp(last), (8, ch)), to_head
        )[0:1]
        swing = per_head[:Q] + arow[...] - jnp.transpose(acol[...])
        dld = mmh(tri_u, swing) + mmh(strict, per_head[Q : 2 * Q]) + fixed
        dstep = per_head[2 * Q :] + dld * neg_c
        slope = sigmoid(raw[sl, :].astype(F32) + db[...])
        o_gdt[sl, :] = dstep[:, :heads] * slope
        dgv = dga[...]
        d_b = mm3(jnp.transpose(dgv), cmap) + mm3(xt * to_end, rv, NT)
        d_c = mm3(dgv, bmap) + mm3(gg, sv, NT)
        per = Q // blk
        qs[pl.ds(c * per, per), :, :ns] = d_b.reshape(per, blk, ns)
        qs[pl.ds(c * per, per), :, ns:] = d_c.reshape(per, blk, ns)
        uv = u[sl, :]
        su = sigmoid(uv)
        dus[sl, :] = (sx * dxt + skip_x * gv) * (su * (1.0 + uv * (1.0 - su)))
        rcur[...] = cf[c] + jnp.exp(last) * rv
        return carry

    lax.fori_loop(0, nc, back, 0)

    phase("wait_q")
    def q_copy(k):
        return remote(qs.at[tp_peer(k)], qr.at[my], sm_p, k, "tp", tp_peer(k))

    def a_copy(k):
        return remote(qa.at[my], qa.at[my], sm_a, k, "tp", tp_peer(k))

    edge_x = remote(dus.at[pl.ds(0, 8)], dus.at[pl.ds(rows, 8)], sm_h, 2, "seq", prv)
    edge_b = remote(dub.at[pl.ds(0, 8)], dub.at[pl.ds(rows, 8)], sm_h, 3, "seq", prv)
    for k in range(1, n_tp):
        q_copy(k).start()
    qr[my] = qs[my]
    edge_x.start()
    for k in range(1, n_tp):
        q_copy(k).wait_recv()
    phase("qsum")
    qsum = qr[0].astype(F32)
    for j in range(1, n_tp):
        qsum = qsum + qr[j].astype(F32)
    qa[my] = qsum.astype(BF16)
    for k in range(1, n_tp):
        a_copy(k).start()

    edge_x.wait_recv()

    phase("convbx")
    def conv_back(ref, weights, out, c):
        base = pl.multiple_of(c * Q, Q)
        ext = ref[pl.ds(base, Q + 8), :]
        tail = jnp.where((c < nc - 1) | (me < n_seq - 1), ext[Q:], 0.0)
        ext = jnp.concatenate([ext[:Q], tail], axis=0)
        acc = weights[3:4, :] * ext[:Q]
        for k in range(3):
            acc = acc + weights[k : k + 1, :] * pltpu.roll(ext, Q + 8 - (3 - k), 0)[:Q]
        out[pl.ds(base, Q), :] = acc

    def conv_back_x(c, carry):
        conv_back(dus, cw, o_gx, c)
        return carry

    lax.fori_loop(0, nc, conv_back_x, 0)

    phase("wait_a")
    for k in range(1, n_tp):
        a_copy(k).wait_recv()
    phase("dub")
    ubv = ub[...]
    sb = sigmoid(ubv)
    dub[pl.ds(0, rows), :] = qa[...].reshape(rows, 2 * ns).astype(F32) * (sb * (1.0 + ubv * (1.0 - sb)))
    edge_b.start()

    phase("wait_o")
    for k in range(1, n_tp):
        o_copy(k).wait_recv()
    phase("osum")
    osum = pr[0].astype(F32)
    for j in range(1, n_tp):
        osum = osum + pr[j].astype(F32)
    o_out[...] = osum.astype(BF16)

    phase("convbb")
    edge_b.wait_recv()

    def conv_back_b(c, carry):
        conv_back(dub, cwb, o_gbc, c)
        return carry

    lax.fori_loop(0, nc, conv_back_b, 0)

    phase("wait_g")
    for k in range(1, n_seq):
        g_copy(k).wait_recv()
    phase("gsum")
    gsum = gr[0].astype(F32)
    for j in range(1, n_seq):
        gsum = gsum + gr[j].astype(F32)
    o_gw[...] = gsum

    phase("drain")
    halo_x.wait_send()
    halo_b.wait_send()
    edge_x.wait_send()
    edge_b.wait_send()
    for k in range(1, n_seq):
        for copy in (t_copy, w_copy, s_copy, sb_copy, v_copy, vb_copy, g_copy):
            copy(k).wait_send()
    for k in range(1, n_tp):
        for copy in (d_copy, r_copy, o_copy, q_copy, a_copy):
            copy(k).wait_send()
    phase("")


def solution(mesh):
    n_seq, n_tp = mesh.shape["seq"], mesh.shape["tp"]

    def shards(
        inner_x,
        gate_z,
        proj_bc,
        dt_raw,
        a_log,
        dt_bias,
        d_skip,
        conv_x,
        bias_x,
        conv_bc,
        bias_bc,
        norm_gain,
        w_out,
        d_out,
    ):
        rows, ch = inner_x.shape
        heads = a_log.shape[0]
        ns2 = proj_bc.shape[1]
        ns = ns2 // 2
        nc = rows // Q
        nrow = ns // n_seq
        wrows, drows = w_out.shape[1], d_out.shape[1]
        width = wrows * n_seq
        w_t = w_out.T
        d_t = d_out.T

        def column(v):
            return jnp.pad(v, (0, 16 - heads))[:, None]

        vm = functools.partial(pl.BlockSpec, memory_space=pltpu.VMEM)
        big = pltpu.VMEM((rows, ch), F32)
        chunk_states = pltpu.VMEM((nc, ns, ch), F32)
        slices = pltpu.VMEM((n_seq, nrow, ch), F32)
        sem_s = pltpu.SemaphoreType.DMA((2, n_seq))
        sem_t = pltpu.SemaphoreType.DMA((2, n_tp))
        scratch = [
            pltpu.VMEM((width, ch), BF16),
            pltpu.VMEM((width, rows), BF16),
            pltpu.VMEM((16, ch), BF16),
            pltpu.VMEM((16, ns2), BF16),
            pltpu.VMEM((8, LANES), F32),
            pltpu.VMEM((n_seq, 8, LANES), F32),
            big,
            big,
            pltpu.VMEM((nc, 16, Q), F32),
            big,
            big,
            pltpu.VMEM((rows, ns2), F32),
            pltpu.VMEM((rows, ns2), F32),
            chunk_states,
            chunk_states,
            chunk_states,
            big,
            big,
            big,
            big,
            pltpu.VMEM((rows, ch), BF16),
            pltpu.VMEM((Q, ch), F32),
            pltpu.VMEM((rows + 8, ch), F32),
            pltpu.VMEM((rows + 8, ns2), F32),
            pltpu.VMEM((ns, ch), F32),
            slices,
            slices,
            slices,
            slices,
            slices,
            slices,
            slices,
            slices,
            pltpu.VMEM((8, rows), F32),
            pltpu.VMEM((n_tp, 8, rows), F32),
            pltpu.VMEM((n_tp, drows, rows), BF16),
            pltpu.VMEM((n_tp, drows, rows), BF16),
            pltpu.VMEM((n_seq, wrows, ch), BF16),
            pltpu.VMEM((n_seq, wrows, ch), BF16),
            pltpu.VMEM((n_tp, rows // n_tp, ns2), F32),
            pltpu.VMEM((n_tp, rows // n_tp, ns2), F32),
            pltpu.VMEM((n_tp, rows // n_tp, ns2), BF16),
            pltpu.VMEM((Q, LANES), F32),
            pltpu.VMEM((LANES, Q), F32),
            pltpu.VMEM((Q, Q), F32),
            pltpu.SemaphoreType.DMA((2, 4)),
            sem_s,
            sem_s,
            sem_t,
            sem_s,
            sem_s,
            sem_s,
            sem_s,
            sem_t,
            sem_t,
            sem_s,
            sem_t,
            sem_t,
        ]
        out_t, g_x, g_z, g_bc, g_dt, g_w = pl.pallas_call(
            functools.partial(kernel, (n_seq, n_tp, ch * n_tp)),
            out_shape=[
                jax.ShapeDtypeStruct((drows, rows), BF16),
                jax.ShapeDtypeStruct((rows, ch), F32),
                jax.ShapeDtypeStruct((rows, ch), F32),
                jax.ShapeDtypeStruct((rows, ns2), F32),
                jax.ShapeDtypeStruct((rows, heads), F32),
                jax.ShapeDtypeStruct((wrows, ch), F32),
            ],
            in_specs=[vm()] * 16,
            out_specs=[vm()] * 6,
            scratch_shapes=scratch,
            compiler_params=pltpu.CompilerParams(
                collective_id=0, has_side_effects=True, vmem_limit_bytes=67_043_328
            ),
            name="mixer",
        )(
            inner_x,
            gate_z,
            proj_bc,
            dt_raw,
            w_t,
            d_t,
            conv_x,
            bias_x[None, :],
            conv_bc,
            bias_bc[None, :],
            norm_gain[None, :],
            a_log[None, :],
            dt_bias[None, :],
            d_skip[None, :],
            column(a_log),
            column(dt_bias),
        )
        return out_t.T, g_x, g_z, g_bc, g_dt, g_w.T

    in_specs = (
        P("seq", "tp"),
        P("seq", "tp"),
        P("seq", None),
        P("seq", "tp"),
        P("tp"),
        P("tp"),
        P("tp"),
        P(None, "tp"),
        P("tp"),
        P(),
        P(),
        P("tp"),
        P("tp", "seq"),
        P("seq", "tp"),
    )
    out_specs = (
        P("seq", "tp"),
        P("seq", "tp"),
        P("seq", "tp"),
        P("seq", None),
        P("seq", "tp"),
        P("tp", "seq"),
    )
    return jax.shard_map(
        shards, mesh=mesh, in_specs=in_specs, out_specs=out_specs, check_vma=False
    )
```

profile of v0, /device:TPU:4, one launch (start us, length us, event | category | flops | bytes accessed | tf_op | source)
XLA Modules:
  0.0 169.9 jit_solution(9864617422051396979)
XLA Ops:
  0.6 0.7 pad_bitcast_fusion.1
  1.3 0.7 pad_bitcast_fusion
  1.9 1.3 broadcast_in_dim.24.bx
  3.2 1.3 broadcast_in_dim.26.gain
  4.5 0.7 copy.22.dbc
  5.2 0.7 copy.21.alc
  5.8 1.5 copy.20.raw
  7.3 153.7 %mixer.1 = (bf16[320,512]{1,0:T(8,128)(2,1)}, f32[512,640]{1,0:T(8,128)}, f32[512,640]{1,0:T(8,128)}, f32[512,256]{1,0:T(8,128)}, f32[512,10]{1,0:T(8,128)}, /*index=5*/f32[160,640]{1,0:T(8,128)}) custom-call(bf16[512,640]{1,0:T(8,128)(2,1)} %ix.1, bf16[512,640]{1,0:T(8,128)(2,1)} %gz.1, bf16[512,256]{1,0:T(8,128)(2,1)} %bc.1, bf16[512,10]{1,0:T(8,128)(2,1)} %copy.20.raw, ...), custom_call_target="tpu_custom_call" | custom-call | tf_op jit(solution)/shard_map/mixer/pallas_call | solution.py:730
  161.0 1.7 copy.23
  162.7 1.7 %copy.29 = bf16[512,320]{0,1:T(8,128)(2,1)} copy(bf16[512,320]{0,1:T(8,128)(2,1)} %bitcast.14) | data formatting | bytes 655360
  164.4 0.0 copy-start
  164.4 2.6 %copy.30 = f32[512,640]{1,0:T(8,128)} copy(f32[512,640]{1,0:T(8,128)} %get-tuple-element.31) | data formatting | bytes 2621440
  167.0 0.0 copy-done
  167.0 0.0 copy-start.1
  167.0 0.0 copy-start.2
  167.0 1.1 copy.31
  168.0 0.3 copy-done.1
  168.3 0.8 copy.32
  169.1 0.0 copy-done.2
  169.1 0.8 copy.33
Async XLA Ops:
  164.4 2.6 %copy-start = (f32[512,640]{1,0:T(8,128)S(1)}, f32[512,640]{1,0:T(8,128)}, u32[]{:S(2)}) copy-start(f32[512,640]{1,0:T(8,128)} %get-tuple-element.32) | copy-start | bytes 3932164
  167.0 1.4 copy-start.1
  167.0 2.2 %copy-start.2 = (f32[160,640]{1,0:T(8,128)S(1)}, f32[160,640]{1,0:T(8,128)}, u32[]{:S(2)}) copy-start(f32[160,640]{1,0:T(8,128)} %get-tuple-element.17) | copy-start | bytes 1228804
where the time goes:
time: 170 us
  Pallas kernels  154 us (91%)
  local copies, waits for them, and re-layouts  15.6 us (9%)
    pallas_call x1, Pallas kernels, shards(): pl.pallas_call(functools.partial(kernel, (n_seq, n_tp, ch * n_tp)), out_s...  154 us
    unnamed x13, local copies, waits for them, and re-layouts  10.4 us

commit v1 on v0

--- a/solution.py
+++ b/solution.py
@@ -76,8 +76,6 @@
     al,
     db,
     ds,
-    alc,
-    dbc,
     o_out,
     o_gx,
     o_gz,
@@ -120,15 +118,26 @@
     ts,
     tr,
     pb,
-    pr,
+    pp,
+    po1,
+    po2,
     gb,
-    gr,
+    ga1,
+    ga2,
+    ga3,
+    ga4,
+    gb1,
+    gb2,
+    gb3,
+    gb4,
     qs,
     qr,
     qa,
     arow,
     acol,
     dga,
+    ssq,
+    sm_l,
     sm_h,
     sm_d,
     sm_w,
@@ -146,7 +155,7 @@
     n_seq, n_tp, inner = sizes
     rows, ch = ix.shape
     nc = rows // Q
-    heads = ch // HEAD
+    heads = raw.shape[0]
     pairs = ch // PAIR
     ns = bc.shape[1] // 2
     me, my = lax.axis_index("seq"), lax.axis_index("tp")
@@ -162,6 +171,22 @@
         if name:
             scope.append(jax.named_scope(name))
             scope[0].__enter__()
+
+    side = 4
+    zi, xi = lax.div(me, side), lax.rem(me, side)
+    yi, core = lax.div(my, 2), lax.rem(my, 2)
+
+    def step(v, k):
+        return lax.rem(v + k + side, side)
+
+    x_up, x_dn = step(xi, 1), step(xi, -1)
+    z_up, z_dn = step(zi, 1), step(zi, -1)
+    y_up, y_dn = step(yi, 1), step(yi, -1)
+    x_far, z_far, y_far = step(xi, 2), step(zi, 2), step(yi, 2)
+    to_xu, to_xd = zi * side + x_up, zi * side + x_dn
+    to_zu, to_zd = z_up * side + xi, z_dn * side + xi
+    to_yu, to_yd = y_up * 2 + core, y_dn * 2 + core
+    mate = yi * 2 + 1 - core
 
     def seq_peer(k):
         return lax.rem(me + k, n_seq)
@@ -194,22 +219,77 @@
     halo_x.start()
     halo_b.start()
 
-    def w_copy(k):
-        return remote(wt, wfull.at[pl.ds(me * wrows, wrows)], sm_w, k, "seq", seq_peer(k))
-
-    def d_copy(k):
-        return remote(dt, dfull.at[pl.ds(my * drows, drows)], sm_g, k, "tp", tp_peer(k))
-
-    for k in range(1, n_tp):
-        d_copy(k).start()
-    own_w = pltpu.make_async_copy(wt, wfull.at[pl.ds(me * wrows, wrows)], sm_w.at[0, 0])
-    own_d = pltpu.make_async_copy(dt, dfull.at[pl.ds(my * drows, drows)], sm_g.at[0, 0])
+    half = wrows // 2
+    near = 48
+    ra, rb = pl.ds(0, half), pl.ds(half, half)
+    ra1, ra2 = pl.ds(0, near), pl.ds(near, half - near)
+    rb1, rb2 = pl.ds(half, near), pl.ds(half + near, half - near)
+    lo, hi, every = pl.ds(0, 2), pl.ds(2, 2), pl.ds(0, side)
+
+    def w_view(z, x, r):
+        return wfull.at[z, x, r]
+
+    def w_move(i, peer, z, x, r, src=None):
+        return remote(w_view(z, x, r) if src is None else src, w_view(z, x, r), sm_w, i, "seq", peer)
+
+    w_copies = [
+        w_move(0, to_xu, zi, xi, ra, wt.at[ra]),
+        w_move(1, to_xd, zi, xi, ra, wt.at[ra]),
+        w_move(2, to_zu, zi, xi, rb, wt.at[rb]),
+        w_move(3, to_zd, zi, xi, rb, wt.at[rb]),
+        w_move(4, to_xu, zi, x_dn, ra1),
+        w_move(5, to_xd, zi, x_up, ra2),
+        w_move(6, to_zu, z_dn, xi, rb1),
+        w_move(7, to_zd, z_up, xi, rb2),
+        w_move(8, to_zu, zi, every, ra),
+        w_move(9, to_zd, zi, every, ra),
+        w_move(10, to_xu, every, xi, rb),
+        w_move(11, to_xd, every, xi, rb),
+        w_move(12, to_zu, z_dn, lo, ra),
+        w_move(13, to_zd, z_up, hi, ra),
+        w_move(14, to_xu, lo, x_dn, rb),
+        w_move(15, to_xd, hi, x_up, rb),
+    ]
+
+    dhalf = drows // 2
+
+    def d_view(y, c, off=0, size=drows):
+        return dfull.at[pl.ds(pl.multiple_of((y * 2 + c) * drows + off, 32), size)]
+
+    def d_move(i, peer, y, c, off=0, size=drows, src=None):
+        view = d_view(y, c, off, size)
+        return remote(view if src is None else src, view, sm_g, i, "tp", peer)
+
+    d_copies = [
+        d_move(0, to_yu, yi, core, src=dt),
+        d_move(1, to_yd, yi, core, src=dt),
+        d_move(2, mate, yi, core, src=dt),
+        d_move(3, to_yu, y_dn, core, 0, dhalf),
+        d_move(4, to_yd, y_up, core, dhalf, dhalf),
+        d_move(5, mate, y_dn, core),
+        d_move(6, mate, y_up, core),
+        d_move(7, mate, y_far, core),
+    ]
+
+    def start(copies, first, last):
+        for copy in copies[first:last]:
+            copy.start()
+
+    def arrived(copies, first, last):
+        for copy in copies[first:last]:
+            copy.wait_recv()
+
+    start(w_copies, 0, 4)
+    start(d_copies, 0, 3)
+    own_w = pltpu.make_async_copy(wt, wfull.at[zi, xi], sm_l.at[0])
+    own_d = pltpu.make_async_copy(dt, d_view(yi, core), sm_l.at[1])
     own_w.start()
     own_d.start()
 
     phase("steps")
     spread = (iota((LANES, ch), 1) // HEAD == iota((LANES, ch), 0)).astype(F32)
     spread_h = spread[:heads]
+    ident = (iota((heads, heads), 0) == iota((heads, heads), 1)).astype(F32)
     negexp = -jnp.exp(al[...])
     neg_x = mmh(jnp.broadcast_to(negexp, (8, heads)), spread_h)[0:1]
     dtb_x = mmh(jnp.broadcast_to(db[...], (8, heads)), spread_h)[0:1]
@@ -218,18 +298,24 @@
     tri_u = (iota((Q, Q), 0) <= iota((Q, Q), 1)).astype(F32)
     strict = (iota((Q, Q), 0) > iota((Q, Q), 1)).astype(F32)
 
-    ident = (iota((16, heads), 0) == iota((16, heads), 1)).astype(F32)
+    def column(v):
+        return mmh(ident, jnp.broadcast_to(v, (8, heads)), NT)[:, 0:1]
+
+    def in_line(ref):
+        return jnp.concatenate([ref[i : i + 1] for i in range(ref.shape[0])], axis=1)
+
+    dt_col, neg_col = column(db[...]), column(negexp)
+    bias_line, gain_line = in_line(bx), in_line(gain)
 
     def steps(c, total):
         sl = pl.ds(pl.multiple_of(c * Q, Q), Q)
-        r = raw[sl, :]
-        s = softplus(mm(r, spread_h) + dtb_x)
-        ld = s * neg_x
-        cum = mmh(tri, ld)
+        r = raw[:, sl].astype(F32)
+        r_t = jnp.transpose(jnp.concatenate([r, jnp.zeros((LANES - heads, Q), F32)], axis=0))
+        s = softplus(mm(r_t, spread) + dtb_x)
+        cum = mmh(tri, s * neg_x)
         st[sl, :] = s
         lx[sl, :] = cum
-        s_t = softplus(mm(ident, r, NT) + dbc[...])
-        lt[c] = mmh(s_t * -jnp.exp(alc[...]), tri_u)
+        lt[c] = mmh(softplus(r + dt_col) * neg_col, tri_u)
         return total + cum[Q - 1 : Q, :]
 
     total = lax.fori_loop(0, nc, steps, jnp.zeros((1, ch), F32))
@@ -243,6 +329,9 @@
     for k in range(1, n_seq):
         t_copy(k).start()
 
+    phase("wait_w1")
+    arrived(w_copies, 0, 4)
+    start(w_copies, 4, 8)
     phase("wait_halo")
     halo_x.wait_recv()
     halo_b.wait_recv()
@@ -256,18 +345,18 @@
         edge = jnp.where(me > 0, halo[...].astype(F32), 0.0)
         head = jnp.where(c > 0, prev, edge)[8:16]
         ext = jnp.concatenate([head, own], axis=0)
-        acc = bias[...] + weights[3:4, :] * own
+        acc = bias + weights[3:4, :] * own
         for k in range(3):
             acc = acc + weights[k : k + 1, :] * pltpu.roll(ext, Q + 8 - (5 + k), 0)[:Q]
         return acc
 
     def convs(c, carry):
         sl = pl.ds(pl.multiple_of(c * Q, Q), Q)
-        vb = conv_of(bc, hb, cwb, bb, c)
+        vb = conv_of(bc, hb, cwb, bb[...], c)
         ub[sl, :] = vb
         pbc = vb * sigmoid(vb)
         bcv[sl, :] = pbc
-        vx = conv_of(ix, hx, cw, bx, c)
+        vx = conv_of(ix, hx, cw, bias_line, c)
         u[sl, :] = vx
         xv = vx * sigmoid(vx)
         x[sl, :] = xv
@@ -291,8 +380,13 @@
     for k in range(1, n_seq):
         s_copy(k).start()
     sr[me] = se[me]
-    for k in range(1, n_seq):
-        w_copy(k).start()
+    phase("wait_w2")
+    own_w.wait()
+    arrived(w_copies, 4, 8)
+    start(w_copies, 8, 12)
+    phase("wait_d1")
+    arrived(d_copies, 0, 2)
+    start(d_copies, 3, 7)
 
     upper = iota((Q, Q), 0) >= iota((Q, Q), 1)
     lower = iota((Q, Q), 0) <= iota((Q, Q), 1)
@@ -329,38 +423,16 @@
         sb_copy(k).start()
     sin[me] = en[me]
 
-    phase("wait_wd")
+    phase("wait_d2")
     own_d.wait()
-    for k in range(1, n_tp):
-        d_copy(k).wait_recv()
-    own_w.wait()
-    for k in range(1, n_seq):
-        w_copy(k).wait_recv()
-
-    phase("gn")
-    width = wrows * n_seq
-    kb = 512
-
-    def gn_block(b, carry):
-        kk = pl.ds(pl.multiple_of(b * kb, kb), kb)
-        part = mm(jnp.transpose(dfull[kk, :]), wfull[kk, :])
-
-        @pl.when(b == 0)
-        def _():
-            gn[...] = part
-
-        @pl.when(b > 0)
-        def _():
-            gn[...] += part
-
-        return carry
-
-    lax.fori_loop(0, width // kb, gn_block, 0)
-
+    arrived(d_copies, 3, 5)
+    start(d_copies, 7, 8)
+    phase("wait_w3")
+    arrived(w_copies, 8, 12)
+    start(w_copies, 12, 16)
     phase("wait_sb")
     for k in range(1, n_seq):
         sb_copy(k).wait_recv()
-
     phase("combine")
     lane = iota((Q, LANES), 1)
 
@@ -373,14 +445,44 @@
         zv = gz[sl, :].astype(F32)
         gv = mixed * zv * sigmoid(zv)
         gated[sl, :] = gv
-        sq = jnp.sum(gv * gv, axis=1, keepdims=True)
-        ip = jnp.sum(gn[sl, :] * gain[...] * gv, axis=1, keepdims=True)
-        both = jnp.where(lane == 0, sq, jnp.where(lane == 1, ip, 0.0))
-        ts[:, pl.ds(pl.multiple_of(c * Q, Q), Q)] = jnp.transpose(both)[:8]
+        ssq[sl, :] = jnp.sum(gv * gv, axis=1, keepdims=True)
         return jnp.exp(cum[Q - 1 : Q, :]) * state + fr[c]
 
     lax.fori_loop(0, nc, combine, sin[...].reshape(ns, ch))
-
+    phase("wait_wd")
+    arrived(d_copies, 2, 3)
+    arrived(d_copies, 5, 8)
+    arrived(w_copies, 12, 16)
+    phase("gn")
+    kb = wrows * side
+
+    def gn_block(b, carry):
+        kk = pl.ds(pl.multiple_of(b * kb, kb), kb)
+        part = mm(jnp.transpose(dfull[kk, :]), wfull[b].reshape(kb, ch))
+
+        @pl.when(b == 0)
+        def _():
+            gn[...] = part
+
+        @pl.when(b > 0)
+        def _():
+            gn[...] += part
+
+        return carry
+
+    lax.fori_loop(0, side, gn_block, 0)
+    phase("sums")
+
+    def sums(c, carry):
+        sl = pl.ds(pl.multiple_of(c * Q, Q), Q)
+        scaled = gn[sl, :] * gain_line
+        gn[sl, :] = scaled
+        ip = jnp.sum(scaled * gated[sl, :], axis=1, keepdims=True)
+        both = jnp.where(lane == 0, ssq[sl, :], jnp.where(lane == 1, ip, 0.0))
+        ts[:, sl] = jnp.transpose(both)[:8]
+        return carry
+
+    lax.fori_loop(0, nc, sums, 0)
     phase("wait_t")
     def r_copy(k):
         return remote(ts, tr.at[my], sm_t, k, "tp", tp_peer(k))
@@ -402,8 +504,8 @@
         inv = lax.rsqrt(ts2[c][:, 0:1] / inner + EPSILON)
         coef = inv * inv * inv * ts2[c][:, 1:2] / inner
         gv = gated[sl, :]
-        nb[sl, :] = (gv * inv * gain[...]).astype(BF16)
-        gg = inv * (gn[sl, :] * gain[...]) - gv * coef
+        nb[sl, :] = (gv * inv * gain_line).astype(BF16)
+        gg = inv * gn[sl, :] - gv * coef
         zv = gz[sl, :].astype(F32)
         sg = sigmoid(zv)
         o_gz[sl, :] = gg * y[sl, :] * sg * (1.0 + zv * (1.0 - sg))
@@ -429,16 +531,29 @@
     rr[me] = re[me]
 
     phase("outmm")
-    def o_copy(k):
-        return remote(pb.at[tp_peer(k)], pr.at[my], sm_o, k, "tp", tp_peer(k))
-
-    for k in range(1, n_tp):
-        d = tp_peer(k)
-        block = wfull[pl.ds(pl.multiple_of(d * drows, drows), drows), :]
-        pb[d] = mm(block, nb[...], NT).astype(BF16)
-        o_copy(k).start()
-    block = wfull[pl.ds(pl.multiple_of(my * drows, drows), drows), :]
-    pr[my] = mm(block, nb[...], NT).astype(BF16)
+    def share(y0, c0):
+        block = wfull[y0, pl.ds(2 * c0, 2)].reshape(drows, ch)
+        pb[y0, c0] = mm(block, nb[...], NT).astype(BF16)
+
+    def other(j, carry):
+        share(j, 1 - core)
+        return carry
+
+    def same(j, carry):
+        share(j, core)
+        return carry
+
+    o_half1, o_half2 = pl.ds(0, dhalf), pl.ds(dhalf, dhalf)
+    o_copies = [
+        remote(pb.at[every, 1 - core], pp, sm_o, 0, "tp", mate),
+        remote(pb.at[y_far, core, o_half1], po1.at[o_half1], sm_o, 1, "tp", to_yu),
+        remote(pb.at[y_far, core, o_half2], po1.at[o_half2], sm_o, 2, "tp", to_yd),
+        remote(pb.at[y_up, core], po2.at[0], sm_o, 3, "tp", to_yu),
+        remote(pb.at[y_dn, core], po2.at[1], sm_o, 4, "tp", to_yd),
+    ]
+    lax.fori_loop(0, side, other, 0)
+    start(o_copies, 0, 1)
+    lax.fori_loop(0, side, same, 0)
 
     phase("wait_v")
     for k in range(1, n_seq):
@@ -452,16 +567,93 @@
     rin[me] = ren[me]
 
     phase("gradw")
-    def g_copy(k):
-        return remote(gb.at[seq_peer(k)], gr.at[me], sm_v, k, "seq", seq_peer(k))
-
-    for k in range(1, n_seq):
-        d = seq_peer(k)
-        block = dfull[pl.ds(pl.multiple_of(d * wrows, wrows), wrows), :]
-        gb[d] = mm(block, nb[...]).astype(BF16)
-        g_copy(k).start()
-    block = dfull[pl.ds(pl.multiple_of(me * wrows, wrows), wrows), :]
-    gr[me] = mm(block, nb[...]).astype(BF16)
+    g_copies = [
+        remote(gb.at[z_far, lo, ra], ga1.at[lo], sm_v, 0, "seq", to_zu),
+        remote(gb.at[z_far, hi, ra], ga1.at[hi], sm_v, 1, "seq", to_zd),
+        remote(gb.at[lo, x_far, rb], gb1.at[lo], sm_v, 2, "seq", to_xu),
+        remote(gb.at[hi, x_far, rb], gb1.at[hi], sm_v, 3, "seq", to_xd),
+        remote(gb.at[z_up, every, ra], ga2.at[0], sm_v, 4, "seq", to_zu),
+        remote(gb.at[z_dn, every, ra], ga2.at[1], sm_v, 5, "seq", to_zd),
+        remote(gb.at[every, x_up, rb], gb2.at[0], sm_v, 6, "seq", to_xu),
+        remote(gb.at[every, x_dn, rb], gb2.at[1], sm_v, 7, "seq", to_xd),
+        remote(gb.at[zi, x_far, ra1], ga3.at[ra1], sm_v, 8, "seq", to_xu),
+        remote(gb.at[zi, x_far, ra2], ga3.at[ra2], sm_v, 9, "seq", to_xd),
+        remote(gb.at[z_far, xi, rb1], gb3.at[ra1], sm_v, 10, "seq", to_zu),
+        remote(gb.at[z_far, xi, rb2], gb3.at[ra2], sm_v, 11, "seq", to_zd),
+        remote(gb.at[zi, x_up, ra], ga4.at[0], sm_v, 12, "seq", to_xu),
+        remote(gb.at[zi, x_dn, ra], ga4.at[1], sm_v, 13, "seq", to_xd),
+        remote(gb.at[z_up, xi, rb], gb4.at[0], sm_v, 14, "seq", to_zu),
+        remote(gb.at[z_dn, xi, rb], gb4.at[1], sm_v, 15, "seq", to_zd),
+    ]
+
+    def plus(ref, index, *others):
+        total = ref[index].astype(F32)
+        for part in others:
+            total = total + part.astype(F32)
+        ref[index] = total.astype(BF16)
+
+    def g_block(k, carry):
+        b = step(zi, 2 + k)
+        rows_of = pl.ds(pl.multiple_of(b * kb, kb), kb)
+        gb[b] = mm(dfull[rows_of, :], nb[...]).astype(BF16).reshape(side, wrows, ch)
+
+        @pl.when(k == 0)
+        def _():
+            start(g_copies, 0, 2)
+
+        return carry
+
+    lax.fori_loop(0, side, g_block, 0)
+    start(g_copies, 2, 4)
+
+    def g_second():
+        arrived(g_copies, 0, 4)
+        for j in range(2):
+            plus(gb, (z_up, j, ra), ga1[j])
+            plus(gb, (z_dn, 2 + j, ra), ga1[2 + j])
+            plus(gb, (j, x_up, rb), gb1[j])
+            plus(gb, (2 + j, x_dn, rb), gb1[2 + j])
+        start(g_copies, 4, 8)
+
+    def g_third():
+        arrived(g_copies, 4, 8)
+        for j in range(side):
+            plus(gb, (zi, j, ra), ga2[0, j], ga2[1, j])
+            plus(gb, (j, xi, rb), gb2[0, j], gb2[1, j])
+        start(g_copies, 8, 12)
+
+    def g_fourth():
+        arrived(g_copies, 8, 12)
+        plus(gb, (zi, x_up, ra1), ga3[ra1])
+        plus(gb, (zi, x_dn, ra2), ga3[ra2])
+        plus(gb, (z_up, xi, rb1), gb3[ra1])
+        plus(gb, (z_dn, xi, rb2), gb3[ra2])
+        start(g_copies, 12, 16)
+
+    def g_last():
+        arrived(g_copies, 12, 16)
+        o_gw[ra, :] = gb[zi, xi, ra].astype(F32) + ga4[0].astype(F32) + ga4[1].astype(F32)
+        o_gw[rb, :] = gb[zi, xi, rb].astype(F32) + gb4[0].astype(F32) + gb4[1].astype(F32)
+
+    def o_second():
+        arrived(o_copies, 0, 1)
+        for j in range(side):
+            plus(pb, (j, core), pp[j])
+        start(o_copies, 1, 3)
+
+    def o_third():
+        arrived(o_copies, 1, 3)
+        plus(pb, (y_up, core, o_half1), po1[o_half1])
+        plus(pb, (y_dn, core, o_half2), po1[o_half2])
+        start(o_copies, 3, 5)
+
+    def o_last():
+        arrived(o_copies, 3, 5)
+        total = pb[yi, core].astype(F32) + po2[0].astype(F32) + po2[1].astype(F32)
+        o_out[...] = total.astype(BF16)
+
+    phase("o_second")
+    o_second()
 
     phase("wait_vb")
     for k in range(1, n_seq):
@@ -520,8 +712,8 @@
         swing = per_head[:Q] + arow[...] - jnp.transpose(acol[...])
         dld = mmh(tri_u, swing) + mmh(strict, per_head[Q : 2 * Q]) + fixed
         dstep = per_head[2 * Q :] + dld * neg_c
-        slope = sigmoid(raw[sl, :].astype(F32) + db[...])
-        o_gdt[sl, :] = dstep[:, :heads] * slope
+        slope = sigmoid(raw[:, sl].astype(F32) + dt_col)
+        o_gdt[:, sl] = jnp.transpose(dstep)[:heads] * slope
         dgv = dga[...]
         d_b = mm3(jnp.transpose(dgv), cmap) + mm3(xt * to_end, rv, NT)
         d_c = mm3(dgv, bmap) + mm3(gg, sv, NT)
@@ -532,6 +724,15 @@
         su = sigmoid(uv)
         dus[sl, :] = (sx * dxt + skip_x * gv) * (su * (1.0 + uv * (1.0 - su)))
         rcur[...] = cf[c] + jnp.exp(last) * rv
+
+        @pl.when(i == 0)
+        def _():
+            o_third()
+
+        @pl.when(i == 1)
+        def _():
+            g_second()
+
         return carry
 
     lax.fori_loop(0, nc, back, 0)
@@ -549,6 +750,9 @@
         q_copy(k).start()
     qr[my] = qs[my]
     edge_x.start()
+    phase("g_third")
+    g_third()
+    phase("wait_q2")
     for k in range(1, n_tp):
         q_copy(k).wait_recv()
     phase("qsum")
@@ -559,6 +763,11 @@
     for k in range(1, n_tp):
         a_copy(k).start()
 
+    phase("o_last")
+    o_last()
+    phase("g_fourth")
+    g_fourth()
+    phase("wait_e")
     edge_x.wait_recv()
 
     phase("convbx")
@@ -587,15 +796,6 @@
     dub[pl.ds(0, rows), :] = qa[...].reshape(rows, 2 * ns).astype(F32) * (sb * (1.0 + ubv * (1.0 - sb)))
     edge_b.start()
 
-    phase("wait_o")
-    for k in range(1, n_tp):
-        o_copy(k).wait_recv()
-    phase("osum")
-    osum = pr[0].astype(F32)
-    for j in range(1, n_tp):
-        osum = osum + pr[j].astype(F32)
-    o_out[...] = osum.astype(BF16)
-
     phase("convbb")
     edge_b.wait_recv()
 
@@ -605,14 +805,8 @@
 
     lax.fori_loop(0, nc, conv_back_b, 0)
 
-    phase("wait_g")
-    for k in range(1, n_seq):
-        g_copy(k).wait_recv()
-    phase("gsum")
-    gsum = gr[0].astype(F32)
-    for j in range(1, n_seq):
-        gsum = gsum + gr[j].astype(F32)
-    o_gw[...] = gsum
+    phase("g_last")
+    g_last()
 
     phase("drain")
     halo_x.wait_send()
@@ -620,11 +814,13 @@
     edge_x.wait_send()
     edge_b.wait_send()
     for k in range(1, n_seq):
-        for copy in (t_copy, w_copy, s_copy, sb_copy, v_copy, vb_copy, g_copy):
+        for copy in (t_copy, s_copy, sb_copy, v_copy, vb_copy):
             copy(k).wait_send()
     for k in range(1, n_tp):
-        for copy in (d_copy, r_copy, o_copy, q_copy, a_copy):
+        for copy in (r_copy, q_copy, a_copy):
             copy(k).wait_send()
+    for copy in w_copies + d_copies + o_copies + g_copies:
+        copy.wait_send()
     phase("")
 
 
@@ -658,9 +854,6 @@
         w_t = w_out.T
         d_t = d_out.T
 
-        def column(v):
-            return jnp.pad(v, (0, 16 - heads))[:, None]
-
         vm = functools.partial(pl.BlockSpec, memory_space=pltpu.VMEM)
         big = pltpu.VMEM((rows, ch), F32)
         chunk_states = pltpu.VMEM((nc, ns, ch), F32)
@@ -668,7 +861,7 @@
         sem_s = pltpu.SemaphoreType.DMA((2, n_seq))
         sem_t = pltpu.SemaphoreType.DMA((2, n_tp))
         scratch = [
-            pltpu.VMEM((width, ch), BF16),
+            pltpu.VMEM((4, 4, wrows, ch), BF16),
             pltpu.VMEM((width, rows), BF16),
             pltpu.VMEM((16, ch), BF16),
             pltpu.VMEM((16, ns2), BF16),
@@ -676,7 +869,7 @@
             pltpu.VMEM((n_seq, 8, LANES), F32),
             big,
             big,
-            pltpu.VMEM((nc, 16, Q), F32),
+            pltpu.VMEM((nc, heads, Q), F32),
             big,
             big,
             pltpu.VMEM((rows, ns2), F32),
@@ -703,16 +896,29 @@
             slices,
             pltpu.VMEM((8, rows), F32),
             pltpu.VMEM((n_tp, 8, rows), F32),
-            pltpu.VMEM((n_tp, drows, rows), BF16),
-            pltpu.VMEM((n_tp, drows, rows), BF16),
-            pltpu.VMEM((n_seq, wrows, ch), BF16),
-            pltpu.VMEM((n_seq, wrows, ch), BF16),
+            pltpu.VMEM((4, 2, drows, rows), BF16),
+            pltpu.VMEM((4, drows, rows), BF16),
+            pltpu.VMEM((drows, rows), BF16),
+            pltpu.VMEM((2, drows, rows), BF16),
+            pltpu.VMEM((4, 4, wrows, ch), BF16),
+            *[
+                pltpu.VMEM(shape, BF16)
+                for shape in 2
+                * [
+                    (4, wrows // 2, ch),
+                    (2, 4, wrows // 2, ch),
+                    (wrows // 2, ch),
+                    (2, wrows // 2, ch),
+                ]
+            ],
             pltpu.VMEM((n_tp, rows // n_tp, ns2), F32),
             pltpu.VMEM((n_tp, rows // n_tp, ns2), F32),
             pltpu.VMEM((n_tp, rows // n_tp, ns2), BF16),
             pltpu.VMEM((Q, LANES), F32),
             pltpu.VMEM((LANES, Q), F32),
             pltpu.VMEM((Q, Q), F32),
+            pltpu.VMEM((rows, 1), F32),
+            pltpu.SemaphoreType.DMA((2,)),
             pltpu.SemaphoreType.DMA((2, 4)),
             sem_s,
             sem_s,
@@ -734,10 +940,10 @@
                 jax.ShapeDtypeStruct((rows, ch), F32),
                 jax.ShapeDtypeStruct((rows, ch), F32),
                 jax.ShapeDtypeStruct((rows, ns2), F32),
-                jax.ShapeDtypeStruct((rows, heads), F32),
+                jax.ShapeDtypeStruct((heads, rows), F32),
                 jax.ShapeDtypeStruct((wrows, ch), F32),
             ],
-            in_specs=[vm()] * 16,
+            in_specs=[vm()] * 14,
             out_specs=[vm()] * 6,
             scratch_shapes=scratch,
             compiler_params=pltpu.CompilerParams(
@@ -748,21 +954,19 @@
             inner_x,
             gate_z,
             proj_bc,
-            dt_raw,
+            dt_raw.T,
             w_t,
             d_t,
             conv_x,
-            bias_x[None, :],
+            bias_x.reshape(-1, LANES),
             conv_bc,
             bias_bc[None, :],
-            norm_gain[None, :],
+            norm_gain.reshape(-1, LANES),
             a_log[None, :],
             dt_bias[None, :],
             d_skip[None, :],
-            column(a_log),
-            column(dt_bias),
         )
-        return out_t.T, g_x, g_z, g_bc, g_dt, g_w.T
+        return out_t.T, g_x, g_z, g_bc, g_dt.T, g_w.T
 
     in_specs = (
         P("seq", "tp"),

time: 170 us -> 104 us (0.61)
  the two profiles are of different devices: /device:TPU:4 before, /device:TPU:1 now
where the time goes in v1:
time: 104 us
  Pallas kernels  95.6 us (92%)
  local copies, waits for them, and re-layouts  7.81 us (8%)
    pallas_call x1, Pallas kernels, shards(): pl.pallas_call(functools.partial(kernel, (n_seq, n_tp, ch * n_tp)), out_s...  95.6 us
    unnamed x14, local copies, waits for them, and re-layouts  7.81 us

profile of v1, /device:TPU:1, one launch (start us, length us, event | category | flops | bytes accessed | tf_op | source)
XLA Modules:
  0.0 104.1 jit_solution(10197184869219537875)
XLA Ops:
  0.6 95.6 %mixer.1 = (bf16[320,512]{1,0:T(8,128)(2,1)}, f32[512,640]{1,0:T(8,128)}, f32[512,640]{1,0:T(8,128)}, f32[512,256]{1,0:T(8,128)}, f32[10,512]{1,0:T(8,128)}, /*index=5*/f32[160,640]{1,0:T(8,128)}) custom-call(bf16[512,640]{1,0:T(8,128)(2,1)} %ix.1, bf16[512,640]{1,0:T(8,128)(2,1)} %gz.1, bf16[512,256]{1,0:T(8,128)(2,1)} %bc.1, bf16[10,512]{1,0:T(8,128)(2,1)} %bitcast.17, ...), custom_call_target="tpu_custom_call" | custom-call | tf_op jit(solution)/shard_map/mixer/pallas_call | solution.py:936
  96.3 1.7 %copy.26 = bf16[512,320]{0,1:T(8,128)(2,1)} copy(bf16[512,320]{0,1:T(8,128)(2,1)} %bitcast.14) | data formatting | bytes 655360
  98.0 0.0 copy-start
  98.0 2.6 %copy.27 = f32[512,640]{1,0:T(8,128)} copy(f32[512,640]{1,0:T(8,128)} %get-tuple-element.25) | data formatting | bytes 2621440
  100.5 0.0 copy-done
  100.5 0.0 copy-start.1
  100.5 0.0 copy-start.3
  100.5 0.0 copy-start.2
  100.5 1.1 %copy.28 = f32[512,640]{1,0:T(8,128)} copy(f32[512,640]{1,0:T(8,128)S(1)} %copy-done) | data formatting | bytes 2621440
  101.6 0.3 copy-done.1
  101.9 0.8 copy.29
  102.7 0.0 copy-done.3
  102.7 0.6 copy.30
  103.3 0.0 copy-done.2
  103.3 0.8 copy.31
Async XLA Ops:
  98.0 2.6 %copy-start = (f32[512,640]{1,0:T(8,128)S(1)}, f32[512,640]{1,0:T(8,128)}, u32[]{:S(2)}) copy-start(f32[512,640]{1,0:T(8,128)} %get-tuple-element.26) | copy-start | bytes 3932164
  100.5 1.4 %copy-start.1 = (f32[512,256]{1,0:T(8,128)S(1)}, f32[512,256]{1,0:T(8,128)}, u32[]{:S(2)}) copy-start(f32[512,256]{1,0:T(8,128)} %get-tuple-element.27) | copy-start | bytes 1572868
  100.5 2.2 %copy-start.3 = (f32[10,512]{1,0:T(8,128)S(1)}, f32[10,512]{1,0:T(8,128)}, u32[]{:S(2)}) copy-start(f32[10,512]{1,0:T(8,128)} %get-tuple-element.16) | copy-start | bytes 61444
  100.5 2.8 %copy-start.2 = (f32[160,640]{1,0:T(8,128)S(1)}, f32[160,640]{1,0:T(8,128)}, u32[]{:S(2)}) copy-start(f32[160,640]{1,0:T(8,128)} %get-tuple-element.17) | copy-start | bytes 1228804

commit v2 on v1

v2 whole, which is shorter than its diff:
```python
import functools

import jax
import jax.numpy as jnp
from jax import lax
from jax.experimental import pallas as pl
from jax.experimental.pallas import tpu as pltpu
from jax.sharding import PartitionSpec as P

MESH = pl.DeviceIdType.MESH
F32 = jnp.float32
BF16 = jnp.bfloat16
HIGH = lax.Precision.HIGHEST
EPSILON = 1e-05
NN = ((1,), (0,))
NT = ((1,), (1,))
Q = 128
PAIR = 128
HEAD = 64
LANES = 128


def mm(a, b, dims=NN):
    return lax.dot_general(a.astype(BF16), b.astype(BF16), (dims, ((), ())), preferred_element_type=F32)


def mmh(a, b, dims=NN):
    return lax.dot_general(
        a.astype(F32), b.astype(F32), (dims, ((), ())), precision=HIGH, preferred_element_type=F32
    )


def halves(v):
    high = v.astype(BF16)
    return high, (v - high.astype(F32)).astype(BF16)


def mm3(a, b, dims=NN):
    a0, a1 = halves(a)
    b0, b1 = halves(b)
    return mm(a0, b0, dims) + (mm(a1, b0, dims) + mm(a0, b1, dims))


def parts(v, count):
    out = []
    for _ in range(count):
        piece = v.astype(BF16)
        out.append(piece)
        v = v - piece.astype(F32)
    return out


def iota(shape, dim):
    return lax.broadcasted_iota(jnp.int32, shape, dim)


def sigmoid(v):
    return 1.0 / (1.0 + jnp.exp(-v))


def softplus(v):
    return jnp.maximum(v, 0.0) + jnp.log1p(jnp.exp(-jnp.abs(v)))


def pair_stack(v):
    lane = iota(v.shape, 1)
    return jnp.concatenate(
        [jnp.where(lane < HEAD, v, 0.0), jnp.where(lane >= HEAD, v, 0.0)], axis=0
    )


def kernel(
    sizes,
    ix_in,
    gz_in,
    bc_in,
    raw_in,
    wt,
    dt,
    cw_in,
    bx_in,
    cwb_in,
    bb_in,
    gain_in,
    al_in,
    db_in,
    ds_in,
    out_hbm,
    gx_hbm,
    gz_hbm,
    gbc_hbm,
    gdt_hbm,
    gw_hbm,
    o_out,
    o_gx,
    o_gz,
    o_gbc,
    o_gdt,
    o_gw,
    ix,
    gz,
    bc,
    raw,
    cw,
    bx,
    cwb,
    bb,
    gain,
    al,
    db,
    ds,
    wfull,
    dfull,
    hx,
    hb,
    dsend,
    dbuf,
    st,
    lx,
    lt,
    u,
    x,
    ub,
    bcv,
    fr,
    sst,
    cf,
    y,
    gated,
    gn,
    gm,
    nb,
    dus,
    dub,
    rcur,
    se,
    sr,
    en,
    sin,
    re,
    rr,
    ren,
    rin,
    ts,
    tr,
    pb,
    pp,
    po1,
    po2,
    gb,
    ga1,
    ga2,
    ga3,
    ga4,
    gb1,
    gb2,
    gb3,
    gb4,
    qs,
    qm,
    qr,
    rst,
    qa,
    arow,
    acol,
    dga,
    invs,
    swings,
    dmap,
    edge,
    sm_m,
    sm_e,
    sm_l,
    sm_h,
    sm_d,
    sm_w,
    sm_g,
    sm_s,
    sm_b,
    sm_r,
    sm_q,
    sm_t,
    sm_o,
    sm_v,
    sm_p,
    sm_a,
):
    n_seq, n_tp, inner = sizes
    rows, ch = ix.shape
    nc = rows // Q
    heads = raw.shape[0]
    pairs = ch // PAIR
    ns = bc.shape[1] // 2
    me, my = lax.axis_index("seq"), lax.axis_index("tp")
    wrows = wt.shape[0]
    drows = 2 * dt.shape[1]
    nrow = ns // n_seq

    scope = []

    def phase(name):
        if scope:
            scope.pop().__exit__(None, None, None)
        if name:
            scope.append(jax.named_scope(name))
            scope[0].__enter__()

    side = 4
    zi, xi = lax.div(me, side), lax.rem(me, side)
    yi, core = lax.div(my, 2), lax.rem(my, 2)

    def step(v, k):
        return lax.rem(v + k + side, side)

    x_up, x_dn = step(xi, 1), step(xi, -1)
    z_up, z_dn = step(zi, 1), step(zi, -1)
    y_up, y_dn = step(yi, 1), step(yi, -1)
    x_far, z_far, y_far = step(xi, 2), step(zi, 2), step(yi, 2)
    to_xu, to_xd = zi * side + x_up, zi * side + x_dn
    to_zu, to_zd = z_up * side + xi, z_dn * side + xi
    to_yu, to_yd = y_up * 2 + core, y_dn * 2 + core
    mate = yi * 2 + 1 - core

    def seq_peer(k):
        return lax.rem(me + k, n_seq)

    def tp_peer(k):
        return lax.rem(my + k, n_tp)

    phase("barrier1")
    barrier = pltpu.get_barrier_semaphore()
    for k in range(1, n_seq):
        pl.semaphore_signal(barrier, inc=1, device_id={"seq": seq_peer(k)}, device_id_type=MESH)
    for k in range(1, n_tp):
        pl.semaphore_signal(barrier, inc=1, device_id={"tp": tp_peer(k)}, device_id_type=MESH)

    def remote(src, dst, sems, k, axis, peer):
        return pltpu.make_async_remote_copy(
            src_ref=src,
            dst_ref=dst,
            send_sem=sems.at[0, k],
            recv_sem=sems.at[1, k],
            device_id={axis: peer},
            device_id_type=MESH,
        )

    nxt, prv = seq_peer(1), seq_peer(n_seq - 1)

    @pl.when(my > 0)
    def _():
        pl.semaphore_signal(barrier, inc=1, device_id={"seq": nxt, "tp": 0}, device_id_type=MESH)

    staged = [
        (raw_in, raw),
        (al_in, al),
        (db_in, db),
        (ds_in, ds),
        (wt, wfull.at[zi, xi]),
        (dt, dfull.at[yi, pl.ds(2 * core, 2)]),
        (ix_in, ix),
        (bc_in, bc),
        (cw_in, cw),
        (bx_in, bx),
        (cwb_in, cwb),
        (bb_in, bb),
        (gain_in, gain),
        (gz_in, gz),
    ]
    loads = [pltpu.make_async_copy(a, b, sm_l.at[i]) for i, (a, b) in enumerate(staged)]
    for load in loads:
        load.start()
    results = [(o_gz, gz_hbm), (o_out, out_hbm), (o_gx, gx_hbm), (o_gw, gw_hbm), (o_gbc, gbc_hbm), (o_gdt, gdt_hbm)]
    stores = [pltpu.make_async_copy(a, b, sm_l.at[14 + i]) for i, (a, b) in enumerate(results)]
    phase("staging")
    for load in loads[:9]:
        load.wait()
    phase("barrier")
    pl.semaphore_wait(barrier, n_seq + n_tp - 2 + jnp.where(my == 0, n_tp - 1, 0))

    phase("start")
    halo_x = remote(ix.at[pl.ds(rows - 16, 16)], hx, sm_h, 0, "seq", nxt)
    halo_b = remote(bc.at[pl.ds(rows - 16, 16)], hb, sm_h, 1, "seq", nxt)
    halo_x.start()
    halo_b.start()

    half = wrows // 2
    near = 48
    ra, rb = pl.ds(0, half), pl.ds(half, half)
    ra1, ra2 = pl.ds(0, near), pl.ds(near, half - near)
    rb1, rb2 = pl.ds(half, near), pl.ds(half + near, half - near)
    lo, hi, every = pl.ds(0, 2), pl.ds(2, 2), pl.ds(0, side)

    def w_view(z, x, r):
        return wfull.at[z, x, r]

    def w_move(i, peer, z, x, r, src=None):
        return remote(w_view(z, x, r) if src is None else src, w_view(z, x, r), sm_w, i, "seq", peer)

    w_copies = [
        w_move(0, to_xu, zi, xi, ra),
        w_move(1, to_xd, zi, xi, ra),
        w_move(2, to_zu, zi, xi, rb),
        w_move(3, to_zd, zi, xi, rb),
        w_move(4, to_zu, zi, xi, ra),
        w_move(5, to_zd, zi, xi, ra),
        w_move(6, to_xu, zi, xi, rb),
        w_move(7, to_xd, zi, xi, rb),
        w_move(8, to_xu, zi, x_dn, ra1),
        w_move(9, to_xd, zi, x_up, ra2),
        w_move(10, to_zu, z_dn, xi, rb1),
        w_move(11, to_zd, z_up, xi, rb2),
        w_move(12, to_zu, zi, x_up, ra),
        w_move(13, to_zd, zi, x_up, ra),
        w_move(14, to_xu, z_up, xi, rb),
        w_move(15, to_xd, z_up, xi, rb),
        w_move(16, to_zu, zi, x_dn, ra),
        w_move(17, to_zd, zi, x_dn, ra),
        w_move(18, to_xu, z_dn, xi, rb),
        w_move(19, to_xd, z_dn, xi, rb),
        w_move(20, to_zu, zi, x_far, ra),
        w_move(21, to_zd, zi, x_far, ra),
        w_move(22, to_xu, z_far, xi, rb),
        w_move(23, to_xd, z_far, xi, rb),
        w_move(24, to_zu, z_dn, lo, ra),
        w_move(25, to_zd, z_up, hi, ra),
        w_move(26, to_xu, lo, x_dn, rb),
        w_move(27, to_xd, hi, x_up, rb),
    ]

    dhalf = drows // 2

    def d_view(y, c, off=0, size=drows):
        if size == drows:
            return dfull.at[y, pl.ds(2 * c, 2)]
        return dfull.at[y, 2 * c + off // size]

    def d_move(i, peer, y, c, off=0, size=drows, src=None):
        view = d_view(y, c, off, size)
        return remote(view if src is None else src, view, sm_g, i, "tp", peer)

    d_copies = [
        d_move(0, to_yu, yi, core),
        d_move(1, to_yd, yi, core),
        d_move(2, mate, yi, core),
        d_move(3, to_yu, y_dn, core, 0, dhalf),
        d_move(4, to_yd, y_up, core, dhalf, dhalf),
        d_move(5, mate, y_dn, core),
        d_move(6, mate, y_up, core),
        d_move(7, mate, y_far, core),
    ]

    def start(copies, first, last):
        for copy in copies[first:last]:
            copy.start()

    def arrived(copies, first, last):
        for copy in copies[first:last]:
            copy.wait_recv()

    start(w_copies, 0, 8)
    start(d_copies, 0, 3)

    phase("steps")
    def spread_of(first):
        return (iota((LANES, ch), 1) // HEAD + first == iota((LANES, ch), 0)).astype(BF16)

    ident = (iota((heads, heads), 0) == iota((heads, heads), 1)).astype(F32)
    spread_s = jnp.concatenate([spread_of(0)] * 3, axis=0)
    spread_l = jnp.concatenate([spread_of(16)] * 3, axis=0)
    spread_h = spread_of(0)[:heads].astype(F32)
    negexp = -jnp.exp(al[...])
    skip_x = mmh(jnp.broadcast_to(ds[...], (8, heads)), spread_h)[0:1]
    tri_u = (iota((Q, Q), 0) <= iota((Q, Q), 1)).astype(F32)

    def column(v):
        return mmh(ident, jnp.broadcast_to(v, (8, heads)), NT)[:, 0:1]

    def in_line(ref):
        return jnp.concatenate([ref[i : i + 1] for i in range(ref.shape[0])], axis=1)

    dt_col, neg_col = column(db[...]), column(negexp)

    for load in loads[9:]:
        load.wait()
    bias_line, gain_line = in_line(bx), in_line(gain)

    def steps(c, total):
        sl = pl.ds(pl.multiple_of(c * Q, Q), Q)
        s_c = softplus(raw[:, sl].astype(F32) + dt_col)
        cum = mmh(s_c * neg_col, tri_u)
        lt[c] = cum
        stacked = jnp.concatenate(
            [
                s_c,
                jnp.zeros((16 - heads, Q), F32),
                cum,
                jnp.zeros((LANES - 16 - heads, Q), F32),
            ],
            axis=0,
        )
        turned = jnp.transpose(stacked)
        pieces = jnp.concatenate(parts(turned, 3), axis=1)
        st[sl, :] = mm(pieces, spread_s)
        lx[sl, :] = mm(pieces, spread_l)
        return total + turned[Q - 1 : Q, :]

    total = lax.fori_loop(0, nc, steps, jnp.zeros((1, LANES), F32))
    dsend[...] = jnp.broadcast_to(total, (8, LANES))
    dbuf[me] = dsend[...]

    def t_copy(k):
        return remote(dsend, dbuf.at[me], sm_d, k, "seq", seq_peer(k))

    for k in range(1, n_seq):
        t_copy(k).start()

    phase("convs")
    def conv_of(ref, halo, weights, bias, c):
        base = pl.multiple_of(c * Q, Q)
        own = ref[pl.ds(base, Q), :].astype(F32)
        if halo is None:
            head = ref[pl.ds(pl.multiple_of(c * Q - 16, 16), 16), :].astype(F32)[8:16]
        else:
            head = jnp.where(me > 0, halo[...].astype(F32), 0.0)[8:16]
        ext = jnp.concatenate([head, own], axis=0)
        acc = bias + weights[3:4, :] * own
        for k in range(3):
            acc = acc + weights[k : k + 1, :] * pltpu.roll(ext, Q + 8 - (5 + k), 0)[:Q]
        return acc

    def convs(c, carry, edge_of=(None, None)):
        sl = pl.ds(pl.multiple_of(c * Q, Q), Q)
        vb = conv_of(bc, edge_of[0], cwb, bb[...], c)
        ub[sl, :] = vb
        pbc = vb * sigmoid(vb)
        bcv[sl, :] = pbc
        vx = conv_of(ix, edge_of[1], cw, bias_line, c)
        u[sl, :] = vx
        xv = vx * sigmoid(vx)
        x[sl, :] = xv
        cum = lx[sl, :]
        to_end = jnp.exp(cum[Q - 1 : Q, :] - cum)
        b_t = jnp.transpose(pbc[:, :ns])
        fresh = mm3(b_t, xv * st[sl, :] * to_end)
        fr[c] = fresh
        return carry

    lax.fori_loop(1, nc, convs, 0)
    phase("wait_halo")
    halo_x.wait_recv()
    halo_b.wait_recv()
    phase("conv0")
    convs(0, 0, (hb, hx))
    end = fr[0]
    for c in range(1, nc):
        end = jnp.exp(lx[pl.ds(c * Q + Q - 1, 1), :]) * end + fr[c]
    se[...] = end.reshape(n_seq, nrow, ch)

    phase("send_s")
    def s_copy(k):
        return remote(se.at[seq_peer(k)], sr.at[me], sm_s, k, "seq", seq_peer(k))

    def sb_copy(k):
        return remote(en.at[seq_peer(k)], sin.at[me], sm_b, k, "seq", seq_peer(k))

    for k in range(1, n_seq):
        s_copy(k).start()
    sr[me] = se[me]
    phase("wait_w1")
    arrived(w_copies, 0, 4)
    start(w_copies, 8, 20)

    upper = iota((Q, Q), 0) >= iota((Q, Q), 1)
    lower = iota((Q, Q), 0) <= iota((Q, Q), 1)

    phase("inside")
    def inside(c, carry):
        sl = pl.ds(pl.multiple_of(c * Q, Q), Q)
        scores = mm3(bcv[sl, ns:], bcv[sl, :ns], NT)
        for p in range(pairs):
            ps = slice(p * PAIR, (p + 1) * PAIR)
            both = []
            for h in (2 * p, 2 * p + 1):
                diff = lx[sl, h * HEAD : h * HEAD + 1] - lt[c, h : h + 1, :]
                decay = jnp.exp(jnp.where(upper, diff, -1e30))
                both.append(decay * scores)
            y[sl, ps] = mm3(jnp.concatenate(both, axis=1), pair_stack(x[sl, ps] * st[sl, ps]))
        return carry

    lax.fori_loop(0, nc, inside, 0)
    phase("wait_w2")
    arrived(w_copies, 8, 12)
    start(w_copies, 20, 24)
    phase("wait_d1")
    arrived(d_copies, 0, 2)
    start(d_copies, 3, 7)

    phase("wait_s")
    for k in range(1, n_seq):
        t_copy(k).wait_recv()
    for k in range(1, n_seq):
        s_copy(k).wait_recv()
    phase("scan")
    fade = jnp.exp(mm(jnp.concatenate(parts(dbuf[:, 0, :], 3), axis=1), spread_l))

    acc = jnp.zeros((nrow, ch), F32)
    for j in range(n_seq):
        en[j] = acc
        acc = fade[j : j + 1] * acc + sr[j]
    for k in range(1, n_seq):
        sb_copy(k).start()
    sin[me] = en[me]

    phase("wait_d2")
    arrived(d_copies, 3, 5)
    start(d_copies, 7, 8)
    phase("wait_w3")
    arrived(w_copies, 4, 8)
    arrived(w_copies, 12, 24)
    start(w_copies, 24, 28)
    phase("wait_sb")
    for k in range(1, n_seq):
        sb_copy(k).wait_recv()
    phase("combine")
    lane = iota((Q, LANES), 1)

    def to_row(i, c, v):
        ts[i, :, pl.ds(pl.multiple_of(c * Q, Q), Q)] = jnp.transpose(jnp.where(lane == 0, v, 0.0))[:8]

    def to_column(row, c):
        block = jnp.concatenate([row[:, c * Q : (c + 1) * Q], jnp.zeros((Q - 8, Q), F32)], axis=0)
        return jnp.transpose(block)[:, 0:1]

    def combine(c, state):
        sl = pl.ds(pl.multiple_of(c * Q, Q), Q)
        sst[c] = state
        cum = lx[sl, :]
        mixed = y[sl, :] + jnp.exp(cum) * mm3(bcv[sl, ns:], state) + skip_x * x[sl, :]
        y[sl, :] = mixed
        zv = gz[sl, :].astype(F32)
        gv = mixed * zv * sigmoid(zv)
        gated[sl, :] = gv
        to_row(0, c, jnp.sum(gv * gv, axis=1, keepdims=True))
        return jnp.exp(cum[Q - 1 : Q, :]) * state + fr[c]

    lax.fori_loop(0, nc, combine, sin[...].reshape(ns, ch))

    def r_copies(i):
        return [
            remote(ts.at[i], tr.at[i, my], sm_t, i * n_tp + k, "tp", tp_peer(k)) for k in range(1, n_tp)
        ]

    def r_total(i):
        total = tr[i, 0]
        for j in range(1, n_tp):
            total = total + tr[i, j]
        return total

    r_squares, r_inner = r_copies(0), r_copies(1)
    start(r_squares, 0, n_tp - 1)
    tr[0, my] = ts[0]

    phase("wait_d")
    arrived(d_copies, 2, 3)
    arrived(d_copies, 5, 8)
    phase("gn")
    kb = wrows * side

    def gn_add(part, first):
        @pl.when(first)
        def _():
            gn[...] = part

        @pl.when(jnp.logical_not(first))
        def _():
            gn[...] += part

    def gn_early(k, carry):
        zz, xx = step(zi, k - 1), step(xi, k - 1)
        d_rows = jnp.concatenate(
            [dfull[zz, :, ra].reshape(kb // 2, rows), dfull[:, xx, rb].reshape(kb // 2, rows)], axis=0
        )
        w_rows = jnp.concatenate(
            [wfull[zz, :, ra].reshape(kb // 2, ch), wfull[:, xx, rb].reshape(kb // 2, ch)], axis=0
        )
        gn_add(mm(jnp.transpose(d_rows), w_rows), k == 0)
        return carry

    lax.fori_loop(0, 3, gn_early, 0)

    phase("wait_ss")
    arrived(r_squares, 0, n_tp - 1)
    inv_row = lax.rsqrt(r_total(0) / inner + EPSILON)
    phase("nb")
    for c in range(nc):
        sl = pl.ds(c * Q, Q)
        inv = to_column(inv_row, c)
        invs[sl, :] = inv
        nb[sl, :] = (gated[sl, :] * inv * gain_line).astype(BF16)
    phase("gradw")
    g_copies = [
        remote(gb.at[z_far, lo, ra], ga1.at[lo], sm_v, 0, "seq", to_zu),
        remote(gb.at[z_far, hi, ra], ga1.at[hi], sm_v, 1, "seq", to_zd),
        remote(gb.at[lo, x_far, rb], gb1.at[lo], sm_v, 2, "seq", to_xu),
        remote(gb.at[hi, x_far, rb], gb1.at[hi], sm_v, 3, "seq", to_xd),
        remote(gb.at[z_up, hi, ra], ga2.at[0, hi], sm_v, 4, "seq", to_zu),
        remote(gb.at[z_dn, lo, ra], ga2.at[1, lo], sm_v, 5, "seq", to_zd),
        remote(gb.at[hi, x_up, rb], gb2.at[0, hi], sm_v, 6, "seq", to_xu),
        remote(gb.at[lo, x_dn, rb], gb2.at[1, lo], sm_v, 7, "seq", to_xd),
        remote(gb.at[z_up, lo, ra], ga2.at[0, lo], sm_v, 8, "seq", to_zu),
        remote(gb.at[z_dn, hi, ra], ga2.at[1, hi], sm_v, 9, "seq", to_zd),
        remote(gb.at[lo, x_up, rb], gb2.at[0, lo], sm_v, 10, "seq", to_xu),
        remote(gb.at[hi, x_dn, rb], gb2.at[1, hi], sm_v, 11, "seq", to_xd),
        remote(gb.at[zi, x_far, ra1], ga3.at[ra1], sm_v, 12, "seq", to_xu),
        remote(gb.at[zi, x_far, ra2], ga3.at[ra2], sm_v, 13, "seq", to_xd),
        remote(gb.at[z_far, xi, rb1], gb3.at[ra1], sm_v, 14, "seq", to_zu),
        remote(gb.at[z_far, xi, rb2], gb3.at[ra2], sm_v, 15, "seq", to_zd),
        remote(gb.at[zi, x_up, ra], ga4.at[0], sm_v, 16, "seq", to_xu),
        remote(gb.at[zi, x_dn, ra], ga4.at[1], sm_v, 17, "seq", to_xd),
        remote(gb.at[z_up, xi, rb], gb4.at[0], sm_v, 18, "seq", to_zu),
        remote(gb.at[z_dn, xi, rb], gb4.at[1], sm_v, 19, "seq", to_zd),
    ]

    def plus(ref, index, *others):
        total = ref[index].astype(F32)
        for part in others:
            total = total + part.astype(F32)
        ref[index] = total.astype(BF16)

    def g_block(k, carry):
        b = step(zi, 2 + k)
        gb[b] = mm(dfull[b].reshape(kb, rows), nb[...]).astype(BF16).reshape(side, wrows, ch)

        @pl.when(k == 0)
        def _():
            start(g_copies, 0, 2)

        return carry

    lax.fori_loop(0, side, g_block, 0)
    start(g_copies, 2, 8)

    def g_second():
        arrived(g_copies, 0, 4)
        for j in range(2):
            plus(gb, (z_up, j, ra), ga1[j])
            plus(gb, (z_dn, 2 + j, ra), ga1[2 + j])
            plus(gb, (j, x_up, rb), gb1[j])
            plus(gb, (2 + j, x_dn, rb), gb1[2 + j])
        start(g_copies, 8, 12)

    def g_third():
        arrived(g_copies, 4, 12)
        for j in range(side):
            plus(gb, (zi, j, ra), ga2[0, j], ga2[1, j])
            plus(gb, (j, xi, rb), gb2[0, j], gb2[1, j])
        start(g_copies, 12, 16)

    def g_fourth():
        arrived(g_copies, 12, 16)
        plus(gb, (zi, x_up, ra1), ga3[ra1])
        plus(gb, (zi, x_dn, ra2), ga3[ra2])
        plus(gb, (z_up, xi, rb1), gb3[ra1])
        plus(gb, (z_dn, xi, rb2), gb3[ra2])
        start(g_copies, 16, 20)

    def g_last():
        arrived(g_copies, 16, 20)
        o_gw[ra, :] = gb[zi, xi, ra].astype(F32) + ga4[0].astype(F32) + ga4[1].astype(F32)
        o_gw[rb, :] = gb[zi, xi, rb].astype(F32) + gb4[0].astype(F32) + gb4[1].astype(F32)

    def o_second():
        arrived(o_copies, 0, 1)
        for j in range(side):
            plus(pb, (j, core), pp[j])
        start(o_copies, 1, 3)

    def o_third():
        arrived(o_copies, 1, 3)
        plus(pb, (y_up, core, o_half1), po1[o_half1])
        plus(pb, (y_dn, core, o_half2), po1[o_half2])
        start(o_copies, 3, 5)

    def o_last():
        arrived(o_copies, 3, 5)
        total = pb[yi, core].astype(F32) + po2[0].astype(F32) + po2[1].astype(F32)
        o_out[...] = total.astype(BF16)
    phase("wait_w4")
    arrived(w_copies, 24, 28)
    phase("gn_last")
    gn_early(3, 0)
    phase("ip")

    def inner_sums(c, carry):
        sl = pl.ds(pl.multiple_of(c * Q, Q), Q)
        scaled = gn[sl, :] * gain_line
        gn[sl, :] = scaled
        to_row(1, c, jnp.sum(scaled * gated[sl, :], axis=1, keepdims=True))
        return carry

    lax.fori_loop(0, nc, inner_sums, 0)
    start(r_inner, 0, n_tp - 1)
    tr[1, my] = ts[1]
    phase("outmm")
    def share(y0, c0):
        block = wfull[y0, pl.ds(2 * c0, 2)].reshape(drows, ch)
        pb[y0, c0] = mm(block, nb[...], NT).astype(BF16)

    def other(j, carry):
        share(j, 1 - core)
        return carry

    def same(j, carry):
        share(j, core)
        return carry

    o_half1, o_half2 = pl.ds(0, dhalf), pl.ds(dhalf, dhalf)
    o_copies = [
        remote(pb.at[every, 1 - core], pp, sm_o, 0, "tp", mate),
        remote(pb.at[y_far, core, o_half1], po1.at[o_half1], sm_o, 1, "tp", to_yu),
        remote(pb.at[y_far, core, o_half2], po1.at[o_half2], sm_o, 2, "tp", to_yd),
        remote(pb.at[y_up, core], po2.at[0], sm_o, 3, "tp", to_yu),
        remote(pb.at[y_dn, core], po2.at[1], sm_o, 4, "tp", to_yd),
    ]
    lax.fori_loop(0, side, other, 0)
    start(o_copies, 0, 1)
    lax.fori_loop(0, side, same, 0)
    phase("wait_ip")
    arrived(r_inner, 0, n_tp - 1)
    ip_row = r_total(1) / inner * inv_row * inv_row * inv_row
    phase("norm")
    for c in range(nc):
        sl = pl.ds(c * Q, Q)
        gg = invs[sl, :] * gn[sl, :] - gated[sl, :] * to_column(ip_row, c)
        zv = gz[sl, :].astype(F32)
        sg = sigmoid(zv)
        o_gz[sl, :] = gg * y[sl, :] * sg * (1.0 + zv * (1.0 - sg))
        gmv = gg * zv * sg
        gm[sl, :] = gmv
        c_t = jnp.transpose(bcv[sl, ns:])
        cf[c] = mm3(c_t, gmv * jnp.exp(lx[sl, :]))

    racc = cf[nc - 1]
    for c in reversed(range(nc - 1)):
        racc = cf[c] + jnp.exp(lx[pl.ds(c * Q + Q - 1, 1), :]) * racc
    re[...] = racc.reshape(n_seq, nrow, ch)

    phase("send_v")
    def v_copy(k):
        return remote(re.at[seq_peer(k)], rr.at[me], sm_r, k, "seq", seq_peer(k))

    def vb_copy(k):
        return remote(ren.at[seq_peer(k)], rin.at[me], sm_q, k, "seq", seq_peer(k))

    for k in range(1, n_seq):
        v_copy(k).start()
    rr[me] = re[me]
    stores[0].start()
    phase("g_second")
    g_second()
    phase("o_second")
    o_second()
    phase("intra")
    def back_inside(c, carry):
        sl = pl.ds(pl.multiple_of(c * Q, Q), Q)
        bmap, cmap = bcv[sl, :ns], bcv[sl, ns:]
        scores = mm3(cmap, bmap, NT)
        scores_t = mm3(bmap, cmap, NT)
        arow[...] = jnp.zeros((Q, LANES), F32)
        acol[...] = jnp.zeros((LANES, Q), F32)
        dga[...] = jnp.zeros((Q, Q), F32)
        for p in range(pairs):
            ps = slice(p * PAIR, (p + 1) * PAIR)
            g2 = gm[sl, ps]
            cross = mm3(g2, pair_stack(x[sl, ps] * st[sl, ps]), NT)
            both = []
            for i_h, h in enumerate((2 * p, 2 * p + 1)):
                diff = lx[sl, h * HEAD : h * HEAD + 1] - lt[c, h : h + 1, :]
                weighted = jnp.exp(jnp.where(upper, diff, -1e30)) * cross[:, i_h * Q : (i_h + 1) * Q]
                dga[...] += weighted
                term = weighted * scores
                arow[...] += jnp.where(lane == h, jnp.sum(term, axis=1, keepdims=True), 0.0)
                acol[h : h + 1, :] = jnp.sum(term, axis=0, keepdims=True)
                decay_t = jnp.exp(jnp.where(lower, lt[c, h : h + 1, :] - lx[sl, h * HEAD : h * HEAD + 1], -1e30))
                both.append((decay_t * scores_t).astype(BF16))
            y[sl, ps] = mm(jnp.concatenate(both, axis=1), pair_stack(g2))
        dgv = dga[...]
        swings[c] = arow[...] - jnp.transpose(acol[...])
        dmap[sl, :ns] = mm3(jnp.transpose(dgv), cmap)
        dmap[sl, ns:] = mm3(dgv, bmap)
        return carry

    def back_insides(first):
        def one(i, carry):
            return back_inside(first - i, carry)

        lax.fori_loop(0, nc // 2, one, 0)

    back_insides(nc - 1)
    back_insides(nc // 2 - 1)

    phase("wait_v")
    for k in range(1, n_seq):
        v_copy(k).wait_recv()
    acc = jnp.zeros((nrow, ch), F32)
    for j in reversed(range(n_seq)):
        ren[j] = acc
        acc = fade[j : j + 1] * acc + rr[j]
    for k in range(1, n_seq):
        vb_copy(k).start()
    rin[me] = ren[me]
    phase("o_third")
    o_third()
    phase("forward_part")
    to_head = (lax.rem(iota((2 * ch, LANES), 0), ch) // HEAD == iota((2 * ch, LANES), 1)).astype(BF16)
    neg_c = jnp.concatenate([negexp, jnp.zeros((1, LANES - heads), F32)], axis=1)
    blk = Q // n_tp
    tail_sum = jnp.concatenate([tri_u.astype(BF16)] * 3, axis=1)
    head_sum = jnp.concatenate([(iota((Q, Q), 0) > iota((Q, Q), 1)).astype(BF16)] * 3, axis=1)

    def by_head(v):
        return mm(jnp.concatenate(parts(v, 2), axis=1), to_head)

    def reads(c, carry):
        sl = pl.ds(pl.multiple_of(c * Q, Q), Q)
        cmap = bcv[sl, ns:]
        sv = sst[c]
        gg = gm[sl, :] * jnp.exp(lx[sl, :])
        dmap[sl, ns:] += mm3(gg, sv, NT)
        swings[c] += by_head(gg * mm(cmap, sv))
        return carry

    lax.fori_loop(0, nc, reads, 0)
    phase("g_third")
    g_third()


    phase("wait_vb")
    for k in range(1, n_seq):
        vb_copy(k).wait_recv()
    phase("inter")
    rcur[...] = rin[...].reshape(ns, ch)
    def m_copy(c):
        return remote(qs.at[c, every, 1 - core], qm.at[c], sm_m, c, "tp", mate)

    def q_copy(c, k):
        y1 = step(yi, k)
        return remote(qs.at[c, y1, core], qr.at[c, yi], sm_p, c * side + k, "tp", y1 * 2 + core)

    def q_send(c):
        m_copy(c).wait_recv()
        for j in range(side):
            qs[c, j, core] += qm[c, j]
        for k in range(1, side):
            q_copy(c, k).start()
        qr[c, yi] = qs[c, yi, core]

    def back_b(i, carry):
        c = nc - 1 - i
        sl = pl.ds(pl.multiple_of(c * Q, Q), Q)
        cum = lx[sl, :]
        last = cum[Q - 1 : Q, :]
        rv = rcur[...]
        rst[c] = rv
        d_b = dmap[sl, :ns] + mm3(x[sl, :] * st[sl, :] * jnp.exp(last - cum), rv, NT)
        qs[c, :, :, :, :ns] = d_b.reshape(side, 2, blk, ns)
        qs[c, :, :, :, ns:] = dmap[sl, ns:].reshape(side, 2, blk, ns)
        rcur[...] = cf[c] + jnp.exp(last) * rv
        m_copy(c).start()

        @pl.when(i > 0)
        def _():
            q_send(c + 1)

        return carry

    lax.fori_loop(0, nc, back_b, 0)
    phase("g_fourth")
    g_fourth()
    phase("inter2")

    def back(i, carry):
        c = i
        sl = pl.ds(pl.multiple_of(c * Q, Q), Q)
        cum = lx[sl, :]
        last = cum[Q - 1 : Q, :]
        rv = rst[c]
        xv = x[sl, :]
        sx = st[sl, :]
        d_in = mm(bcv[sl, :ns], rv) * jnp.exp(last - cum)
        dxt = y[sl, :] + d_in
        uv = u[sl, :]
        su = sigmoid(uv)
        dus[sl, :] = (sx * dxt + skip_x * gm[sl, :]) * (su * (1.0 + uv * (1.0 - su)))
        per_head = by_head(jnp.concatenate([xv * sx * d_in, xv * dxt], axis=0))
        fixed = by_head(
            jnp.broadcast_to(jnp.sum(rv * sst[c], axis=0, keepdims=True) * jnp.exp(last), (8, ch))
        )[0:1]
        dld = (
            mm(tail_sum, jnp.concatenate(parts(swings[c], 3), axis=0))
            + mm(head_sum, jnp.concatenate(parts(per_head[:Q], 3), axis=0))
            + fixed
        )
        dstep = per_head[Q:] + dld * neg_c
        slope = sigmoid(raw[:, sl].astype(F32) + dt_col)
        o_gdt[:, sl] = jnp.transpose(dstep)[:heads] * slope

        @pl.when(i == 0)
        def _():
            q_send(0)
            edge_x.start()

        return carry

    edge_x = remote(dus.at[pl.ds(0, 8)], dus.at[pl.ds(rows, 8)], sm_h, 2, "seq", prv)
    lax.fori_loop(0, nc, back, 0)
    stores[5].start()
    phase("wait_q")

    def a_copy(k):
        return remote(qa.at[my], qa.at[my], sm_a, k, "tp", tp_peer(k))

    def edge_b(j):
        return pltpu.make_async_remote_copy(
            src_ref=edge,
            dst_ref=dub.at[pl.ds(rows, 8)],
            send_sem=sm_e.at[j],
            recv_sem=sm_h.at[1, 3],
            device_id={"seq": prv, "tp": j},
            device_id_type=MESH,
        )

    for c in range(nc):
        for k in range(1, side):
            q_copy(c, k).wait_recv()
    phase("qsum")
    qsum = qr[:, 0]
    for j in range(1, side):
        qsum = qsum + qr[:, j]
    qa[my] = qsum.astype(BF16)
    ube = ub[pl.ds(0, 8), :]
    sbe = sigmoid(ube)
    edge[...] = qsum[0, 0:8, :] * (sbe * (1.0 + ube * (1.0 - sbe)))

    @pl.when(my == 0)
    def _():
        for j in range(n_tp):
            edge_b(j).start()

    for k in range(1, n_tp):
        a_copy(k).start()

    phase("o_last")
    o_last()
    phase("wait_e")
    edge_x.wait_recv()

    phase("convbx")
    def conv_back(ref, weights, out, c):
        base = pl.multiple_of(c * Q, Q)
        ext = ref[pl.ds(base, Q + 8), :]
        tail = jnp.where((c < nc - 1) | (me < n_seq - 1), ext[Q:], 0.0)
        ext = jnp.concatenate([ext[:Q], tail], axis=0)
        acc = weights[3:4, :] * ext[:Q]
        for k in range(3):
            acc = acc + weights[k : k + 1, :] * pltpu.roll(ext, Q + 8 - (3 - k), 0)[:Q]
        out[pl.ds(base, Q), :] = acc

    def conv_back_x(c, carry):
        conv_back(dus, cw, o_gx, c)
        return carry

    lax.fori_loop(0, nc, conv_back_x, 0)

    stores[1].start()
    stores[2].start()
    phase("g_last")
    g_last()
    phase("wait_a")
    for k in range(1, n_tp):
        a_copy(k).wait_recv()
    phase("dub")
    for c in range(nc):
        sl = pl.ds(c * Q, Q)
        ubv = ub[sl, :]
        sb = sigmoid(ubv)
        dub[sl, :] = qa[:, c].reshape(Q, 2 * ns).astype(F32) * (sb * (1.0 + ubv * (1.0 - sb)))

    phase("convbb")
    edge_b(0).wait_recv()

    def conv_back_b(c, carry):
        conv_back(dub, cwb, o_gbc, c)
        return carry

    stores[3].start()
    lax.fori_loop(0, nc, conv_back_b, 0)
    stores[4].start()

    phase("drain")
    halo_x.wait_send()
    halo_b.wait_send()
    edge_x.wait_send()

    @pl.when(my == 0)
    def _():
        for j in range(n_tp):
            edge_b(j).wait_send()

    for k in range(1, n_seq):
        for copy in (t_copy, s_copy, sb_copy, v_copy, vb_copy):
            copy(k).wait_send()
    for k in range(1, n_tp):
        a_copy(k).wait_send()
    for c in range(nc):
        m_copy(c).wait_send()
        for k in range(1, side):
            q_copy(c, k).wait_send()
    for copy in r_squares + r_inner:
        copy.wait_send()
    for copy in w_copies + d_copies + o_copies + g_copies:
        copy.wait_send()
    for store in stores:
        store.wait()
    phase("")


def solution(mesh):
    n_seq, n_tp = mesh.shape["seq"], mesh.shape["tp"]

    def shards(
        inner_x,
        gate_z,
        proj_bc,
        dt_raw,
        a_log,
        dt_bias,
        d_skip,
        conv_x,
        bias_x,
        conv_bc,
        bias_bc,
        norm_gain,
        w_out,
        d_out,
    ):
        rows, ch = inner_x.shape
        heads = a_log.shape[0]
        ns2 = proj_bc.shape[1]
        ns = ns2 // 2
        nc = rows // Q
        nrow = ns // n_seq
        wrows, drows = w_out.shape[1], d_out.shape[1]
        w_t = w_out.T
        d_t = d_out.T.reshape(2, drows // 2, rows)

        big = pltpu.VMEM((rows, ch), F32)
        chunk_states = pltpu.VMEM((nc, ns, ch), F32)
        slices = pltpu.VMEM((n_seq, nrow, ch), F32)
        sem_s = pltpu.SemaphoreType.DMA((2, n_seq))
        sem_t = pltpu.SemaphoreType.DMA((2, n_tp))
        scratch = [
            pltpu.VMEM((drows, rows), BF16),
            big,
            big,
            pltpu.VMEM((rows, ns2), F32),
            pltpu.VMEM((heads, rows), F32),
            pltpu.VMEM((wrows, ch), F32),
            pltpu.VMEM((rows, ch), BF16),
            pltpu.VMEM((rows, ch), BF16),
            pltpu.VMEM((rows, ns2), BF16),
            pltpu.VMEM((heads, rows), BF16),
            pltpu.VMEM((4, ch), F32),
            pltpu.VMEM((ch // LANES, LANES), F32),
            pltpu.VMEM((4, ns2), F32),
            pltpu.VMEM((1, ns2), F32),
            pltpu.VMEM((ch // LANES, LANES), F32),
            pltpu.VMEM((1, heads), F32),
            pltpu.VMEM((1, heads), F32),
            pltpu.VMEM((1, heads), F32),
            pltpu.VMEM((4, 4, wrows, ch), BF16),
            pltpu.VMEM((4, 4, wrows, rows), BF16),
            pltpu.VMEM((16, ch), BF16),
            pltpu.VMEM((16, ns2), BF16),
            pltpu.VMEM((8, LANES), F32),
            pltpu.VMEM((n_seq, 8, LANES), F32),
            big,
            big,
            pltpu.VMEM((nc, heads, Q), F32),
            big,
            big,
            pltpu.VMEM((rows, ns2), F32),
            pltpu.VMEM((rows, ns2), F32),
            chunk_states,
            chunk_states,
            chunk_states,
            big,
            big,
            big,
            big,
            pltpu.VMEM((rows, ch), BF16),
            pltpu.VMEM((rows + 8, ch), F32),
            pltpu.VMEM((rows + 8, ns2), F32),
            pltpu.VMEM((ns, ch), F32),
            slices,
            slices,
            slices,
            slices,
            slices,
            slices,
            slices,
            slices,
            pltpu.VMEM((2, 8, rows), F32),
            pltpu.VMEM((2, n_tp, 8, rows), F32),
            pltpu.VMEM((4, 2, drows, rows), BF16),
            pltpu.VMEM((4, drows, rows), BF16),
            pltpu.VMEM((drows, rows), BF16),
            pltpu.VMEM((2, drows, rows), BF16),
            pltpu.VMEM((4, 4, wrows, ch), BF16),
            *[
                pltpu.VMEM(shape, BF16)
                for shape in 2
                * [
                    (4, wrows // 2, ch),
                    (2, 4, wrows // 2, ch),
                    (wrows // 2, ch),
                    (2, wrows // 2, ch),
                ]
            ],
            pltpu.VMEM((nc, 4, 2, Q // n_tp, ns2), F32),
            pltpu.VMEM((nc, 4, Q // n_tp, ns2), F32),
            pltpu.VMEM((nc, 4, Q // n_tp, ns2), F32),
            chunk_states,
            pltpu.VMEM((n_tp, nc, Q // n_tp, ns2), BF16),
            pltpu.VMEM((Q, LANES), F32),
            pltpu.VMEM((LANES, Q), F32),
            pltpu.VMEM((Q, Q), F32),
            pltpu.VMEM((rows, 1), F32),
            pltpu.VMEM((nc, Q, LANES), F32),
            pltpu.VMEM((rows, ns2), F32),
            pltpu.VMEM((8, ns2), F32),
            pltpu.SemaphoreType.DMA((2, nc)),
            pltpu.SemaphoreType.DMA((n_tp,)),
            pltpu.SemaphoreType.DMA((20,)),
            pltpu.SemaphoreType.DMA((2, 4)),
            sem_s,
            pltpu.SemaphoreType.DMA((2, 28)),
            sem_t,
            sem_s,
            sem_s,
            sem_s,
            sem_s,
            pltpu.SemaphoreType.DMA((2, 2 * n_tp)),
            sem_t,
            pltpu.SemaphoreType.DMA((2, 20)),
            pltpu.SemaphoreType.DMA((2, nc * n_tp)),
            sem_t,
        ]
        out_t, g_x, g_z, g_bc, g_dt, g_w = pl.pallas_call(
            functools.partial(kernel, (n_seq, n_tp, ch * n_tp)),
            out_shape=[
                jax.ShapeDtypeStruct((drows, rows), BF16),
                jax.ShapeDtypeStruct((rows, ch), F32),
                jax.ShapeDtypeStruct((rows, ch), F32),
                jax.ShapeDtypeStruct((rows, ns2), F32),
                jax.ShapeDtypeStruct((heads, rows), F32),
                jax.ShapeDtypeStruct((wrows, ch), F32),
            ],
            in_specs=[pl.BlockSpec(memory_space=pltpu.HBM)] * 14,
            out_specs=[pl.BlockSpec(memory_space=pltpu.HBM)] * 6,
            scratch_shapes=scratch,
            compiler_params=pltpu.CompilerParams(
                collective_id=0, has_side_effects=True, vmem_limit_bytes=62 * 1024 * 1024
            ),
            name="mixer",
        )(
            inner_x,
            gate_z,
            proj_bc,
            dt_raw.T,
            w_t,
            d_t,
            conv_x,
            bias_x.reshape(-1, LANES),
            conv_bc,
            bias_bc[None, :],
            norm_gain.reshape(-1, LANES),
            a_log[None, :],
            dt_bias[None, :],
            d_skip[None, :],
        )
        return out_t.T, g_x, g_z, g_bc, g_dt.T, g_w.T

    in_specs = (
        P("seq", "tp"),
        P("seq", "tp"),
        P("seq", None),
        P("seq", "tp"),
        P("tp"),
        P("tp"),
        P("tp"),
        P(None, "tp"),
        P("tp"),
        P(),
        P(),
        P("tp"),
        P("tp", "seq"),
        P("seq", "tp"),
    )
    out_specs = (
        P("seq", "tp"),
        P("seq", "tp"),
        P("seq", "tp"),
        P("seq", None),
        P("seq", "tp"),
        P("tp", "seq"),
    )
    return jax.shard_map(
        shards, mesh=mesh, in_specs=in_specs, out_specs=out_specs, check_vma=False
    )
```

time: 104 us -> 91.8 us (0.88)
  Pallas kernels: 95.6 us -> 83.1 us
    pallas_call x1, Pallas kernels: 95.6 us -> 83.1 us  [shards(): pl.pallas_call(functools.partial(kernel, (n_seq, n_tp, ch * n_tp)), out_s...]
where the time goes in v2:
time: 91.8 us; the launch traced here: 91.6 us
  Pallas kernels  83.1 us (91%)
  local copies, waits for them, and re-layouts  7.81 us (9%)
    pallas_call x1, Pallas kernels, shards(): pl.pallas_call(functools.partial(kernel, (n_seq, n_tp, ch * n_tp)), out_s...  83.1 us
    unnamed x14, local copies, waits for them, and re-layouts  7.81 us

profile of v2, /device:TPU:1, one launch (start us, length us, event | category | flops | bytes accessed | tf_op | source)
XLA Modules:
  0.0 91.6 jit_solution(898411244705821487)
XLA Ops:
  0.6 83.1 %mixer.1 = (bf16[320,512]{1,0:T(8,128)(2,1)}, f32[512,640]{1,0:T(8,128)}, f32[512,640]{1,0:T(8,128)}, f32[512,256]{1,0:T(8,128)}, f32[10,512]{1,0:T(8,128)}, /*index=5*/f32[160,640]{1,0:T(8,128)}) custom-call(bf16[512,640]{1,0:T(8,128)(2,1)} %ix_in.1, bf16[512,640]{1,0:T(8,128)(2,1)} %gz_in.1, bf16[512,256]{1,0:T(8,128)(2,1)} %bc_in.1, ...), custom_call_target="tpu_custom_call" | custom-call | tf_op jit(solution)/shard_map/mixer/pallas_call | solution.py:1159
  83.8 1.7 %copy.26 = bf16[512,320]{0,1:T(8,128)(2,1)} copy(bf16[512,320]{0,1:T(8,128)(2,1)} %bitcast.16) | data formatting | bytes 655360
  85.5 0.0 copy-start
  85.5 2.6 %copy.27 = f32[512,640]{1,0:T(8,128)} copy(f32[512,640]{1,0:T(8,128)} %get-tuple-element.25) | data formatting | bytes 2621440
  88.0 0.0 copy-done
  88.0 0.0 copy-start.1
  88.0 0.0 copy-start.3
  88.0 0.0 copy-start.2
  88.0 1.1 %copy.28 = f32[512,640]{1,0:T(8,128)} copy(f32[512,640]{1,0:T(8,128)S(1)} %copy-done) | data formatting | bytes 2621440
  89.1 0.3 copy-done.1
  89.4 0.8 copy.29
  90.2 0.0 copy-done.3
  90.2 0.6 copy.30
  90.8 0.0 copy-done.2
  90.8 0.8 copy.31
Async XLA Ops:
  85.5 2.6 %copy-start = (f32[512,640]{1,0:T(8,128)S(1)}, f32[512,640]{1,0:T(8,128)}, u32[]{:S(2)}) copy-start(f32[512,640]{1,0:T(8,128)} %get-tuple-element.26) | copy-start | bytes 3932164
  88.0 1.4 %copy-start.1 = (f32[512,256]{1,0:T(8,128)S(1)}, f32[512,256]{1,0:T(8,128)}, u32[]{:S(2)}) copy-start(f32[512,256]{1,0:T(8,128)} %get-tuple-element.27) | copy-start | bytes 1572868
  88.0 2.2 %copy-start.3 = (f32[10,512]{1,0:T(8,128)S(1)}, f32[10,512]{1,0:T(8,128)}, u32[]{:S(2)}) copy-start(f32[10,512]{1,0:T(8,128)} %get-tuple-element.16) | copy-start | bytes 61444
  88.0 2.8 %copy-start.2 = (f32[160,640]{1,0:T(8,128)S(1)}, f32[160,640]{1,0:T(8,128)}, u32[]{:S(2)}) copy-start(f32[160,640]{1,0:T(8,128)} %get-tuple-element.17) | copy-start | bytes 1228804

commit v3 on v2

--- a/solution.py
+++ b/solution.py
@@ -221,8 +221,15 @@
     to_yu, to_yd = y_up * 2 + core, y_dn * 2 + core
     mate = yi * 2 + 1 - core
 
+    def hops(pair):
+        return sum(min(v, side - v) for v in pair)
+
+    others = [(a, b) for a in range(side) for b in range(side) if a or b]
+    others.sort(key=lambda pair: -hops(pair))
+
     def seq_peer(k):
-        return lax.rem(me + k, n_seq)
+        a, b = others[k - 1]
+        return step(zi, a) * side + step(xi, b)
 
     def tp_peer(k):
         return lax.rem(my + k, n_tp)
@@ -244,7 +251,7 @@
             device_id_type=MESH,
         )
 
-    nxt, prv = seq_peer(1), seq_peer(n_seq - 1)
+    nxt, prv = lax.rem(me + 1, n_seq), lax.rem(me + n_seq - 1, n_seq)
 
     @pl.when(my > 0)
     def _():
@@ -468,7 +475,7 @@
     sr[me] = se[me]
     phase("wait_w1")
     arrived(w_copies, 0, 4)
-    start(w_copies, 8, 20)
+    start(w_copies, 8, 16)
 
     upper = iota((Q, Q), 0) >= iota((Q, Q), 1)
     lower = iota((Q, Q), 0) <= iota((Q, Q), 1)
@@ -488,13 +495,9 @@
         return carry
 
     lax.fori_loop(0, nc, inside, 0)
-    phase("wait_w2")
-    arrived(w_copies, 8, 12)
-    start(w_copies, 20, 24)
     phase("wait_d1")
     arrived(d_copies, 0, 2)
     start(d_copies, 3, 7)
-
     phase("wait_s")
     for k in range(1, n_seq):
         t_copy(k).wait_recv()
@@ -510,14 +513,11 @@
     for k in range(1, n_seq):
         sb_copy(k).start()
     sin[me] = en[me]
-
-    phase("wait_d2")
-    arrived(d_copies, 3, 5)
-    start(d_copies, 7, 8)
-    phase("wait_w3")
-    arrived(w_copies, 4, 8)
-    arrived(w_copies, 12, 24)
-    start(w_copies, 24, 28)
+    start(w_copies, 16, 20)
+    phase("wait_w2")
+    arrived(w_copies, 8, 12)
+    start(w_copies, 20, 24)
+
     phase("wait_sb")
     for k in range(1, n_seq):
         sb_copy(k).wait_recv()
@@ -560,6 +560,13 @@
     start(r_squares, 0, n_tp - 1)
     tr[0, my] = ts[0]
 
+    phase("wait_d2")
+    arrived(d_copies, 3, 5)
+    start(d_copies, 7, 8)
+    phase("wait_w3")
+    arrived(w_copies, 4, 8)
+    arrived(w_copies, 12, 24)
+    start(w_copies, 24, 28)
     phase("wait_d")
     arrived(d_copies, 2, 3)
     arrived(d_copies, 5, 8)
@@ -825,16 +832,18 @@
         sl = pl.ds(pl.multiple_of(c * Q, Q), Q)
         cmap = bcv[sl, ns:]
         sv = sst[c]
-        gg = gm[sl, :] * jnp.exp(lx[sl, :])
+        cum = lx[sl, :]
+        gg = gm[sl, :] * jnp.exp(cum)
+        gn[sl, :] = x[sl, :] * st[sl, :] * jnp.exp(cum[Q - 1 : Q, :] - cum)
         dmap[sl, ns:] += mm3(gg, sv, NT)
         swings[c] += by_head(gg * mm(cmap, sv))
         return carry
 
     lax.fori_loop(0, nc, reads, 0)
+
+
     phase("g_third")
     g_third()
-
-
     phase("wait_vb")
     for k in range(1, n_seq):
         vb_copy(k).wait_recv()
@@ -855,18 +864,28 @@
             q_copy(c, k).start()
         qr[c, yi] = qs[c, yi, core]
 
+    def a_copy(c, k):
+        return remote(qa.at[my, c], qa.at[my, c], sm_a, c * n_tp + k, "tp", tp_peer(k))
+
+    def a_send(c):
+        for k in range(1, side):
+            q_copy(c, k).wait_recv()
+        total = qr[c, 0] + qr[c, 1] + qr[c, 2] + qr[c, 3]
+        qa[my, c] = total.astype(BF16)
+        for k in range(1, n_tp):
+            a_copy(c, k).start()
+        return total
+
     def back_b(i, carry):
         c = nc - 1 - i
         sl = pl.ds(pl.multiple_of(c * Q, Q), Q)
-        cum = lx[sl, :]
-        last = cum[Q - 1 : Q, :]
         rv = rcur[...]
         rst[c] = rv
-        d_b = dmap[sl, :ns] + mm3(x[sl, :] * st[sl, :] * jnp.exp(last - cum), rv, NT)
+        d_b = dmap[sl, :ns] + mm3(gn[sl, :], rv, NT)
         qs[c, :, :, :, :ns] = d_b.reshape(side, 2, blk, ns)
         qs[c, :, :, :, ns:] = dmap[sl, ns:].reshape(side, 2, blk, ns)
-        rcur[...] = cf[c] + jnp.exp(last) * rv
         m_copy(c).start()
+        rcur[...] = cf[c] + jnp.exp(lx[pl.ds(c * Q + Q - 1, 1), :]) * rv
 
         @pl.when(i > 0)
         def _():
@@ -910,15 +929,16 @@
             q_send(0)
             edge_x.start()
 
+        @pl.when(i < nc - 1)
+        def _():
+            a_send(nc - 1 - i)
+
         return carry
 
     edge_x = remote(dus.at[pl.ds(0, 8)], dus.at[pl.ds(rows, 8)], sm_h, 2, "seq", prv)
     lax.fori_loop(0, nc, back, 0)
     stores[5].start()
     phase("wait_q")
-
-    def a_copy(k):
-        return remote(qa.at[my], qa.at[my], sm_a, k, "tp", tp_peer(k))
 
     def edge_b(j):
         return pltpu.make_async_remote_copy(
@@ -930,25 +950,16 @@
             device_id_type=MESH,
         )
 
-    for c in range(nc):
-        for k in range(1, side):
-            q_copy(c, k).wait_recv()
-    phase("qsum")
-    qsum = qr[:, 0]
-    for j in range(1, side):
-        qsum = qsum + qr[:, j]
-    qa[my] = qsum.astype(BF16)
+    qsum = a_send(0)
     ube = ub[pl.ds(0, 8), :]
     sbe = sigmoid(ube)
-    edge[...] = qsum[0, 0:8, :] * (sbe * (1.0 + ube * (1.0 - sbe)))
+    edge[...] = qsum[0:8, :] * (sbe * (1.0 + ube * (1.0 - sbe)))
 
     @pl.when(my == 0)
     def _():
         for j in range(n_tp):
             edge_b(j).start()
 
-    for k in range(1, n_tp):
-        a_copy(k).start()
 
     phase("o_last")
     o_last()
@@ -977,8 +988,9 @@
     phase("g_last")
     g_last()
     phase("wait_a")
-    for k in range(1, n_tp):
-        a_copy(k).wait_recv()
+    for c in range(nc):
+        for k in range(1, n_tp):
+            a_copy(c, k).wait_recv()
     phase("dub")
     for c in range(nc):
         sl = pl.ds(c * Q, Q)
@@ -1010,10 +1022,10 @@
     for k in range(1, n_seq):
         for copy in (t_copy, s_copy, sb_copy, v_copy, vb_copy):
             copy(k).wait_send()
-    for k in range(1, n_tp):
-        a_copy(k).wait_send()
     for c in range(nc):
         m_copy(c).wait_send()
+        for k in range(1, n_tp):
+            a_copy(c, k).wait_send()
         for k in range(1, side):
             q_copy(c, k).wait_send()
     for copy in r_squares + r_inner:
@@ -1023,6 +1035,32 @@
     for store in stores:
         store.wait()
     phase("")
+
+
+def publish(*refs):
+    count = (len(refs) - 2) // 3
+    sources, targets, held = refs[:count], refs[count : 2 * count], refs[2 * count : 3 * count]
+    sem_in, sem_out = refs[-2:]
+    moves = []
+    for source, target, place in zip(sources, targets, held):
+        rows = source.shape[0]
+        pieces = 4 if rows * source.shape[1] > 200_000 else 1
+        for i in range(pieces):
+            part = pl.ds(i * (rows // pieces), rows // pieces)
+            k = len(moves)
+            moves.append(
+                (
+                    pltpu.make_async_copy(source.at[part], place.at[part], sem_in.at[k]),
+                    pltpu.make_async_copy(place.at[part], target.at[part], sem_out.at[k]),
+                )
+            )
+    for load, _ in moves:
+        load.start()
+    for load, store in moves:
+        load.wait()
+        store.start()
+    for _, store in moves:
+        store.wait()
 
 
 def solution(mesh):
@@ -1154,7 +1192,7 @@
             sem_t,
             pltpu.SemaphoreType.DMA((2, 20)),
             pltpu.SemaphoreType.DMA((2, nc * n_tp)),
-            sem_t,
+            pltpu.SemaphoreType.DMA((2, nc * n_tp)),
         ]
         out_t, g_x, g_z, g_bc, g_dt, g_w = pl.pallas_call(
             functools.partial(kernel, (n_seq, n_tp, ch * n_tp)),
@@ -1189,6 +1227,18 @@
             dt_bias[None, :],
             d_skip[None, :],
         )
+        results = (g_x, g_z, g_bc, g_w, out_t, g_dt)
+        hbm = pl.BlockSpec(memory_space=pltpu.HBM)
+        g_x, g_z, g_bc, g_w, out_t, g_dt = pl.pallas_call(
+            publish,
+            out_shape=[jax.ShapeDtypeStruct(v.shape, v.dtype) for v in results],
+            in_specs=[hbm] * 6,
+            out_specs=[hbm] * 6,
+            scratch_shapes=[pltpu.VMEM(v.shape, v.dtype) for v in results]
+            + [pltpu.SemaphoreType.DMA((16,)), pltpu.SemaphoreType.DMA((16,))],
+            compiler_params=pltpu.CompilerParams(vmem_limit_bytes=62 * 1024 * 1024),
+            name="publish",
+        )(*results)
         return out_t.T, g_x, g_z, g_bc, g_dt.T, g_w.T
 
     in_specs = (

time: 91.8 us -> 82.4 us (0.90)
  local copies, waits for them, and re-layouts: 7.81 us -> 0 us
  Pallas kernels: 83.1 us -> 81.4 us
    unnamed x14 -> x0, local copies, waits for them, and re-layouts: 7.81 us -> none
    pallas_call x1, Pallas kernels: 83.1 us -> 77.9 us  [shards(): pl.pallas_call(functools.partial(kernel, (n_seq, n_tp, ch * n_tp)), out_s...]
    pallas_call x0 -> x1, Pallas kernels: none -> 3.51 us  [shards(): pl.pallas_call(publish, out_shape=[jax.ShapeDtypeStruct(v.shape, v.dtype)...]
where the time goes in v3:
time: 82.4 us; the launch traced here: 82.2 us
  Pallas kernels  81.4 us (99%)
    pallas_call x1, Pallas kernels, shards(): pl.pallas_call(functools.partial(kernel, (n_seq, n_tp, ch * n_tp)), out_s...  77.9 us
    pallas_call x1, Pallas kernels, shards(): pl.pallas_call(publish, out_shape=[jax.ShapeDtypeStruct(v.shape, v.dtype)...  3.51 us

profile of v3, /device:TPU:1, one launch (start us, length us, event | category | flops | bytes accessed | tf_op | source)
XLA Modules:
  0.0 82.2 jit_solution(17226916381784694302)
XLA Ops:
  0.6 77.9 %mixer.1 = (bf16[320,512]{1,0:T(8,128)(2,1)}, f32[512,640]{1,0:T(8,128)}, f32[512,640]{1,0:T(8,128)}, f32[512,256]{1,0:T(8,128)}, f32[10,512]{1,0:T(8,128)}, /*index=5*/f32[160,640]{1,0:T(8,128)}) custom-call(bf16[512,640]{1,0:T(8,128)(2,1)} %ix_in.1, bf16[512,640]{1,0:T(8,128)(2,1)} %gz_in.1, bf16[512,256]{1,0:T(8,128)(2,1)} %bc_in.1, ...), custom_call_target="tpu_custom_call" | custom-call | tf_op jit(solution)/shard_map/mixer/pallas_call | solution.py:1197
  78.6 3.5 %publish.1 = (f32[512,640]{1,0:T(8,128)}, f32[512,640]{1,0:T(8,128)}, f32[512,256]{1,0:T(8,128)}, f32[160,640]{1,0:T(8,128)}, bf16[320,512]{1,0:T(8,128)(2,1)}, /*index=5*/f32[10,512]{1,0:T(8,128)}) custom-call(f32[512,640]{1,0:T(8,128)} %get-tuple-element.18.refs_0_, f32[512,640]{1,0:T(8,128)} %get-tuple-element.19.refs_1_, ...), custom_call_target="tpu_custom_call" | custom-call | tf_op jit(solution)/shard_map/publish/pallas_call | solution.py:1232

commit v4 on v3

--- a/solution.py
+++ b/solution.py
@@ -168,6 +168,8 @@
     swings,
     dmap,
     edge,
+    frow,
+    packed,
     sm_m,
     sm_e,
     sm_l,
@@ -218,6 +220,7 @@
     x_far, z_far, y_far = step(xi, 2), step(zi, 2), step(yi, 2)
     to_xu, to_xd = zi * side + x_up, zi * side + x_dn
     to_zu, to_zd = z_up * side + xi, z_dn * side + xi
+    to_xf, to_zf = zi * side + x_far, z_far * side + xi
     to_yu, to_yd = y_up * 2 + core, y_dn * 2 + core
     mate = yi * 2 + 1 - core
 
@@ -368,13 +371,12 @@
     start(d_copies, 0, 3)
 
     phase("steps")
-    def spread_of(first):
-        return (iota((LANES, ch), 1) // HEAD + first == iota((LANES, ch), 0)).astype(BF16)
-
+    slot = lax.rem(iota((LANES, 2 * ch), 0), 32)
+    wanted = iota((LANES, 2 * ch), 1) // HEAD
+    wanted = jnp.where(wanted < heads, wanted, wanted - heads + 16)
+    spread = ((slot == wanted) & (iota((LANES, 2 * ch), 0) < 96)).astype(BF16)
+    spread_h = (iota((heads, ch), 1) // HEAD == iota((heads, ch), 0)).astype(F32)
     ident = (iota((heads, heads), 0) == iota((heads, heads), 1)).astype(F32)
-    spread_s = jnp.concatenate([spread_of(0)] * 3, axis=0)
-    spread_l = jnp.concatenate([spread_of(16)] * 3, axis=0)
-    spread_h = spread_of(0)[:heads].astype(F32)
     negexp = -jnp.exp(al[...])
     skip_x = mmh(jnp.broadcast_to(ds[...], (8, heads)), spread_h)[0:1]
     tri_u = (iota((Q, Q), 0) <= iota((Q, Q), 1)).astype(F32)
@@ -396,22 +398,17 @@
         s_c = softplus(raw[:, sl].astype(F32) + dt_col)
         cum = mmh(s_c * neg_col, tri_u)
         lt[c] = cum
-        stacked = jnp.concatenate(
-            [
-                s_c,
-                jnp.zeros((16 - heads, Q), F32),
-                cum,
-                jnp.zeros((LANES - 16 - heads, Q), F32),
-            ],
-            axis=0,
-        )
-        turned = jnp.transpose(stacked)
-        pieces = jnp.concatenate(parts(turned, 3), axis=1)
-        st[sl, :] = mm(pieces, spread_s)
-        lx[sl, :] = mm(pieces, spread_l)
+        gap = jnp.zeros((16 - heads, Q), F32)
+        pieces = []
+        for a, b in zip(parts(s_c, 3), parts(cum, 3)):
+            pieces += [a.astype(F32), gap, b.astype(F32), gap]
+        turned = jnp.transpose(jnp.concatenate([*pieces, jnp.zeros((LANES - 96, Q), F32)], axis=0))
+        packed[sl, :] = turned.astype(BF16)
         return total + turned[Q - 1 : Q, :]
 
     total = lax.fori_loop(0, nc, steps, jnp.zeros((1, LANES), F32))
+    st[...] = mm(packed[...], spread[:, :ch])
+    lx[...] = mm(packed[...], spread[:, ch:])
     dsend[...] = jnp.broadcast_to(total, (8, LANES))
     dbuf[me] = dsend[...]
 
@@ -504,7 +501,7 @@
     for k in range(1, n_seq):
         s_copy(k).wait_recv()
     phase("scan")
-    fade = jnp.exp(mm(jnp.concatenate(parts(dbuf[:, 0, :], 3), axis=1), spread_l))
+    fade = jnp.exp(sum(mm(piece, spread[:, ch:]) for piece in parts(dbuf[:, 0, :], 3)))
 
     acc = jnp.zeros((nrow, ch), F32)
     for j in range(n_seq):
@@ -614,18 +611,20 @@
         remote(gb.at[z_dn, lo, ra], ga2.at[1, lo], sm_v, 5, "seq", to_zd),
         remote(gb.at[hi, x_up, rb], gb2.at[0, hi], sm_v, 6, "seq", to_xu),
         remote(gb.at[lo, x_dn, rb], gb2.at[1, lo], sm_v, 7, "seq", to_xd),
-        remote(gb.at[z_up, lo, ra], ga2.at[0, lo], sm_v, 8, "seq", to_zu),
-        remote(gb.at[z_dn, hi, ra], ga2.at[1, hi], sm_v, 9, "seq", to_zd),
-        remote(gb.at[lo, x_up, rb], gb2.at[0, lo], sm_v, 10, "seq", to_xu),
-        remote(gb.at[hi, x_dn, rb], gb2.at[1, hi], sm_v, 11, "seq", to_xd),
-        remote(gb.at[zi, x_far, ra1], ga3.at[ra1], sm_v, 12, "seq", to_xu),
-        remote(gb.at[zi, x_far, ra2], ga3.at[ra2], sm_v, 13, "seq", to_xd),
-        remote(gb.at[z_far, xi, rb1], gb3.at[ra1], sm_v, 14, "seq", to_zu),
-        remote(gb.at[z_far, xi, rb2], gb3.at[ra2], sm_v, 15, "seq", to_zd),
-        remote(gb.at[zi, x_up, ra], ga4.at[0], sm_v, 16, "seq", to_xu),
-        remote(gb.at[zi, x_dn, ra], ga4.at[1], sm_v, 17, "seq", to_xd),
-        remote(gb.at[z_up, xi, rb], gb4.at[0], sm_v, 18, "seq", to_zu),
-        remote(gb.at[z_dn, xi, rb], gb4.at[1], sm_v, 19, "seq", to_zd),
+        remote(gb.at[z_up, 0, ra], ga2.at[0, 0], sm_v, 8, "seq", to_zu),
+        remote(gb.at[z_dn, 2, ra], ga2.at[1, 2], sm_v, 9, "seq", to_zd),
+        remote(gb.at[0, x_up, rb], gb2.at[0, 0], sm_v, 10, "seq", to_xu),
+        remote(gb.at[2, x_dn, rb], gb2.at[1, 2], sm_v, 11, "seq", to_xd),
+        remote(gb.at[z_up, 1, ra], ga2.at[0, 1], sm_v, 20, "seq", to_zu),
+        remote(gb.at[z_dn, 3, ra], ga2.at[1, 3], sm_v, 21, "seq", to_zd),
+        remote(gb.at[1, x_up, rb], gb2.at[0, 1], sm_v, 22, "seq", to_xu),
+        remote(gb.at[3, x_dn, rb], gb2.at[1, 3], sm_v, 23, "seq", to_xd),
+        remote(gb.at[zi, x_far, ra], ga3, sm_v, 12, "seq", to_xf),
+        remote(gb.at[z_far, xi, rb], gb3, sm_v, 13, "seq", to_zf),
+        remote(gb.at[zi, x_up, ra], ga4.at[0], sm_v, 14, "seq", to_xu),
+        remote(gb.at[zi, x_dn, ra], ga4.at[1], sm_v, 15, "seq", to_xd),
+        remote(gb.at[z_up, xi, rb], gb4.at[0], sm_v, 16, "seq", to_zu),
+        remote(gb.at[z_dn, xi, rb], gb4.at[1], sm_v, 17, "seq", to_zd),
     ]
 
     def plus(ref, index, *others):
@@ -657,24 +656,20 @@
         start(g_copies, 8, 12)
 
     def g_third():
-        arrived(g_copies, 4, 12)
+        arrived(g_copies, 4, 16)
         for j in range(side):
             plus(gb, (zi, j, ra), ga2[0, j], ga2[1, j])
             plus(gb, (j, xi, rb), gb2[0, j], gb2[1, j])
-        start(g_copies, 12, 16)
-
-    def g_fourth():
-        arrived(g_copies, 12, 16)
-        plus(gb, (zi, x_up, ra1), ga3[ra1])
-        plus(gb, (zi, x_dn, ra2), ga3[ra2])
-        plus(gb, (z_up, xi, rb1), gb3[ra1])
-        plus(gb, (z_dn, xi, rb2), gb3[ra2])
-        start(g_copies, 16, 20)
+        start(g_copies, 16, 22)
 
     def g_last():
-        arrived(g_copies, 16, 20)
-        o_gw[ra, :] = gb[zi, xi, ra].astype(F32) + ga4[0].astype(F32) + ga4[1].astype(F32)
-        o_gw[rb, :] = gb[zi, xi, rb].astype(F32) + gb4[0].astype(F32) + gb4[1].astype(F32)
+        arrived(g_copies, 16, 22)
+
+        def landed(own, far, near):
+            return own.astype(F32) + far.astype(F32) + near[0].astype(F32) + near[1].astype(F32)
+
+        o_gw[ra, :] = landed(gb[zi, xi, ra], ga3[...], ga4)
+        o_gw[rb, :] = landed(gb[zi, xi, rb], gb3[...], gb4)
 
     def o_second():
         arrived(o_copies, 0, 1)
@@ -816,6 +811,7 @@
     for k in range(1, n_seq):
         vb_copy(k).start()
     rin[me] = ren[me]
+    start(g_copies, 12, 16)
     phase("o_third")
     o_third()
     phase("forward_part")
@@ -828,22 +824,27 @@
     def by_head(v):
         return mm(jnp.concatenate(parts(v, 2), axis=1), to_head)
 
-    def reads(c, carry):
+    def reads(i, later):
+        c = nc - 1 - i
         sl = pl.ds(pl.multiple_of(c * Q, Q), Q)
         cmap = bcv[sl, ns:]
         sv = sst[c]
         cum = lx[sl, :]
+        last = cum[Q - 1 : Q, :]
         gg = gm[sl, :] * jnp.exp(cum)
-        gn[sl, :] = x[sl, :] * st[sl, :] * jnp.exp(cum[Q - 1 : Q, :] - cum)
         dmap[sl, ns:] += mm3(gg, sv, NT)
         swings[c] += by_head(gg * mm(cmap, sv))
-        return carry
-
-    lax.fori_loop(0, nc, reads, 0)
-
-
-    phase("g_third")
-    g_third()
+        rv = rcur[...]
+        rst[c] = rv
+        reach = x[sl, :] * st[sl, :] * jnp.exp(last - cum)
+        dmap[sl, :ns] += mm3(reach, rv, NT)
+        gn[sl, :] = reach * later
+        frow[c] = jnp.broadcast_to(later, (8, ch))
+        rcur[...] = cf[c] + jnp.exp(last) * rv
+        return later * jnp.exp(last)
+
+    rcur[...] = jnp.zeros((ns, ch), F32)
+    lax.fori_loop(0, nc, reads, jnp.ones((1, ch), F32))
     phase("wait_vb")
     for k in range(1, n_seq):
         vb_copy(k).wait_recv()
@@ -876,26 +877,15 @@
             a_copy(c, k).start()
         return total
 
-    def back_b(i, carry):
-        c = nc - 1 - i
+    def back_b(c, carry):
         sl = pl.ds(pl.multiple_of(c * Q, Q), Q)
-        rv = rcur[...]
-        rst[c] = rv
-        d_b = dmap[sl, :ns] + mm3(gn[sl, :], rv, NT)
-        qs[c, :, :, :, :ns] = d_b.reshape(side, 2, blk, ns)
+        qs[c, :, :, :, :ns] = dmap[sl, :ns].reshape(side, 2, blk, ns)
         qs[c, :, :, :, ns:] = dmap[sl, ns:].reshape(side, 2, blk, ns)
         m_copy(c).start()
-        rcur[...] = cf[c] + jnp.exp(lx[pl.ds(c * Q + Q - 1, 1), :]) * rv
-
-        @pl.when(i > 0)
-        def _():
-            q_send(c + 1)
-
         return carry
 
+    dmap[:, :ns] += mm3(gn[...], rcur[...], NT)
     lax.fori_loop(0, nc, back_b, 0)
-    phase("g_fourth")
-    g_fourth()
     phase("inter2")
 
     def back(i, carry):
@@ -903,7 +893,7 @@
         sl = pl.ds(pl.multiple_of(c * Q, Q), Q)
         cum = lx[sl, :]
         last = cum[Q - 1 : Q, :]
-        rv = rst[c]
+        rv = rst[c] + frow[c][0:1] * rcur[...]
         xv = x[sl, :]
         sx = st[sl, :]
         d_in = mm(bcv[sl, :ns], rv) * jnp.exp(last - cum)
@@ -926,12 +916,13 @@
 
         @pl.when(i == 0)
         def _():
-            q_send(0)
+            for j in range(nc):
+                q_send(j)
             edge_x.start()
 
-        @pl.when(i < nc - 1)
+        @pl.when(i == 1)
         def _():
-            a_send(nc - 1 - i)
+            g_third()
 
         return carry
 
@@ -951,6 +942,9 @@
         )
 
     qsum = a_send(0)
+    a_send(1)
+    for c in range(2, nc):
+        a_send(c)
     ube = ub[pl.ds(0, 8), :]
     sbe = sigmoid(ube)
     edge[...] = qsum[0:8, :] * (sbe * (1.0 + ube * (1.0 - sbe)))
@@ -1177,6 +1171,8 @@
             pltpu.VMEM((nc, Q, LANES), F32),
             pltpu.VMEM((rows, ns2), F32),
             pltpu.VMEM((8, ns2), F32),
+            pltpu.VMEM((nc, 8, ch), F32),
+            pltpu.VMEM((rows, LANES), BF16),
             pltpu.SemaphoreType.DMA((2, nc)),
             pltpu.SemaphoreType.DMA((n_tp,)),
             pltpu.SemaphoreType.DMA((20,)),
@@ -1190,7 +1186,7 @@
             sem_s,
             pltpu.SemaphoreType.DMA((2, 2 * n_tp)),
             sem_t,
-            pltpu.SemaphoreType.DMA((2, 20)),
+            pltpu.SemaphoreType.DMA((2, 24)),
             pltpu.SemaphoreType.DMA((2, nc * n_tp)),
             pltpu.SemaphoreType.DMA((2, nc * n_tp)),
         ]

time: 82.4 us -> 80.6 us (0.978)
  Pallas kernels: 81.4 us -> 79.7 us
    pallas_call x1, Pallas kernels: 77.9 us -> 76.2 us  [shards(): pl.pallas_call(functools.partial(kernel, (n_seq, n_tp, ch * n_tp)), out_s...]
where the time goes in v4:
time: 80.6 us; the launch traced here: 80.5 us
  Pallas kernels  79.7 us (99%)
  between operations  0.81 us (1%)
    pallas_call x1, Pallas kernels, shards(): pl.pallas_call(functools.partial(kernel, (n_seq, n_tp, ch * n_tp)), out_s...  76.2 us
    pallas_call x1, Pallas kernels, shards(): pl.pallas_call(publish, out_shape=[jax.ShapeDtypeStruct(v.shape, v.dtype)...  3.51 us

profile of v4, /device:TPU:1, one launch (start us, length us, event | category | flops | bytes accessed | tf_op | source)
XLA Modules:
  0.0 80.5 jit_solution(1025510282111497333)
XLA Ops:
  0.6 76.2 %mixer.1 = (bf16[320,512]{1,0:T(8,128)(2,1)}, f32[512,640]{1,0:T(8,128)}, f32[512,640]{1,0:T(8,128)}, f32[512,256]{1,0:T(8,128)}, f32[10,512]{1,0:T(8,128)}, /*index=5*/f32[160,640]{1,0:T(8,128)}) custom-call(bf16[512,640]{1,0:T(8,128)(2,1)} %ix_in.1, bf16[512,640]{1,0:T(8,128)(2,1)} %gz_in.1, bf16[512,256]{1,0:T(8,128)(2,1)} %bc_in.1, ...), custom_call_target="tpu_custom_call" | custom-call | tf_op jit(solution)/shard_map/mixer/pallas_call | solution.py:1193
  76.8 3.5 %publish.1 = (f32[512,640]{1,0:T(8,128)}, f32[512,640]{1,0:T(8,128)}, f32[512,256]{1,0:T(8,128)}, f32[160,640]{1,0:T(8,128)}, bf16[320,512]{1,0:T(8,128)(2,1)}, /*index=5*/f32[10,512]{1,0:T(8,128)}) custom-call(f32[512,640]{1,0:T(8,128)} %get-tuple-element.18.refs_0_, f32[512,640]{1,0:T(8,128)} %get-tuple-element.19.refs_1_, ...), custom_call_target="tpu_custom_call" | custom-call | tf_op jit(solution)/shard_map/publish/pallas_call | solution.py:1228

commit v5 on v4

--- a/solution.py
+++ b/solution.py
@@ -331,10 +331,14 @@
         w_move(21, to_zd, zi, x_far, ra),
         w_move(22, to_xu, z_far, xi, rb),
         w_move(23, to_xd, z_far, xi, rb),
-        w_move(24, to_zu, z_dn, lo, ra),
-        w_move(25, to_zd, z_up, hi, ra),
-        w_move(26, to_xu, lo, x_dn, rb),
-        w_move(27, to_xd, hi, x_up, rb),
+        w_move(24, to_zu, z_dn, xi, ra),
+        w_move(25, to_xu, zi, x_dn, rb),
+        w_move(26, to_zu, z_dn, x_up, ra),
+        w_move(27, to_xu, z_up, x_dn, rb),
+        w_move(28, to_zd, z_up, x_dn, ra),
+        w_move(29, to_xd, z_dn, x_up, rb),
+        w_move(30, to_zd, z_up, x_far, ra),
+        w_move(31, to_xd, z_far, x_up, rb),
     ]
 
     dhalf = drows // 2
@@ -518,6 +522,8 @@
     phase("wait_sb")
     for k in range(1, n_seq):
         sb_copy(k).wait_recv()
+    arrived(d_copies, 3, 5)
+    start(d_copies, 7, 8)
     phase("combine")
     lane = iota((Q, LANES), 1)
 
@@ -557,40 +563,36 @@
     start(r_squares, 0, n_tp - 1)
     tr[0, my] = ts[0]
 
-    phase("wait_d2")
-    arrived(d_copies, 3, 5)
-    start(d_copies, 7, 8)
-    phase("wait_w3")
+    phase("wait_w_near")
     arrived(w_copies, 4, 8)
-    arrived(w_copies, 12, 24)
-    start(w_copies, 24, 28)
-    phase("wait_d")
-    arrived(d_copies, 2, 3)
-    arrived(d_copies, 5, 8)
-    phase("gn")
+    arrived(w_copies, 12, 20)
+    start(w_copies, 24, 30)
+    phase("gn_own")
     kb = wrows * side
 
-    def gn_add(part, first):
-        @pl.when(first)
-        def _():
-            gn[...] = part
-
-        @pl.when(jnp.logical_not(first))
-        def _():
-            gn[...] += part
-
-    def gn_early(k, carry):
-        zz, xx = step(zi, k - 1), step(xi, k - 1)
+    moves = (0, 1, -1, 2)
+
+    def gn_early(k):
+        zz, xx = step(zi, moves[k]), step(xi, moves[k])
         d_rows = jnp.concatenate(
             [dfull[zz, :, ra].reshape(kb // 2, rows), dfull[:, xx, rb].reshape(kb // 2, rows)], axis=0
         )
         w_rows = jnp.concatenate(
             [wfull[zz, :, ra].reshape(kb // 2, ch), wfull[:, xx, rb].reshape(kb // 2, ch)], axis=0
         )
-        gn_add(mm(jnp.transpose(d_rows), w_rows), k == 0)
-        return carry
-
-    lax.fori_loop(0, 3, gn_early, 0)
+        part = mm(jnp.transpose(d_rows), w_rows)
+        gn[...] = part if k == 0 else gn[...] + part
+
+    arrived(d_copies, 2, 3)
+    arrived(d_copies, 5, 7)
+    arrived(d_copies, 7, 8)
+    gn_early(0)
+    phase("wait_w3")
+    arrived(w_copies, 20, 24)
+    start(w_copies, 30, 32)
+    phase("gn")
+    gn_early(1)
+    gn_early(2)
 
     phase("wait_ss")
     arrived(r_squares, 0, n_tp - 1)
@@ -688,9 +690,9 @@
         total = pb[yi, core].astype(F32) + po2[0].astype(F32) + po2[1].astype(F32)
         o_out[...] = total.astype(BF16)
     phase("wait_w4")
-    arrived(w_copies, 24, 28)
+    arrived(w_copies, 24, 32)
     phase("gn_last")
-    gn_early(3, 0)
+    gn_early(3)
     phase("ip")
 
     def inner_sums(c, carry):
@@ -1178,7 +1180,7 @@
             pltpu.SemaphoreType.DMA((20,)),
             pltpu.SemaphoreType.DMA((2, 4)),
             sem_s,
-            pltpu.SemaphoreType.DMA((2, 28)),
+            pltpu.SemaphoreType.DMA((2, 32)),
             sem_t,
             sem_s,
             sem_s,

time: 80.6 us -> 79.8 us (0.990)
  Pallas kernels: 79.7 us -> 78.8 us
    pallas_call x1, Pallas kernels: 76.2 us -> 75.3 us  [shards(): pl.pallas_call(functools.partial(kernel, (n_seq, n_tp, ch * n_tp)), out_s...]
where the time goes in v5:
time: 79.8 us; the launch traced here: 79.6 us
  Pallas kernels  78.8 us (99%)
  between operations  0.81 us (1%)
    pallas_call x1, Pallas kernels, shards(): pl.pallas_call(functools.partial(kernel, (n_seq, n_tp, ch * n_tp)), out_s...  75.3 us
    pallas_call x1, Pallas kernels, shards(): pl.pallas_call(publish, out_shape=[jax.ShapeDtypeStruct(v.shape, v.dtype)...  3.51 us

profile of v5, /device:TPU:1, one launch (start us, length us, event | category | flops | bytes accessed | tf_op | source)
XLA Modules:
  0.0 79.6 jit_solution(11170445259445471055)
XLA Ops:
  0.6 75.3 %mixer.1 = (bf16[320,512]{1,0:T(8,128)(2,1)}, f32[512,640]{1,0:T(8,128)}, f32[512,640]{1,0:T(8,128)}, f32[512,256]{1,0:T(8,128)}, f32[10,512]{1,0:T(8,128)}, /*index=5*/f32[160,640]{1,0:T(8,128)}) custom-call(bf16[512,640]{1,0:T(8,128)(2,1)} %ix_in.1, bf16[512,640]{1,0:T(8,128)(2,1)} %gz_in.1, bf16[512,256]{1,0:T(8,128)(2,1)} %bc_in.1, ...), custom_call_target="tpu_custom_call" | custom-call | tf_op jit(solution)/shard_map/mixer/pallas_call | solution.py:1195
  75.9 3.5 %publish.1 = (f32[512,640]{1,0:T(8,128)}, f32[512,640]{1,0:T(8,128)}, f32[512,256]{1,0:T(8,128)}, f32[160,640]{1,0:T(8,128)}, bf16[320,512]{1,0:T(8,128)(2,1)}, /*index=5*/f32[10,512]{1,0:T(8,128)}) custom-call(f32[512,640]{1,0:T(8,128)} %get-tuple-element.18.refs_0_, f32[512,640]{1,0:T(8,128)} %get-tuple-element.19.refs_1_, ...), custom_call_target="tpu_custom_call" | custom-call | tf_op jit(solution)/shard_map/publish/pallas_call | solution.py:1230

commit v6 on v5

--- a/solution.py
+++ b/solution.py
@@ -981,8 +981,6 @@
 
     stores[1].start()
     stores[2].start()
-    phase("g_last")
-    g_last()
     phase("wait_a")
     for c in range(nc):
         for k in range(1, n_tp):
@@ -1001,9 +999,10 @@
         conv_back(dub, cwb, o_gbc, c)
         return carry
 
-    stores[3].start()
     lax.fori_loop(0, nc, conv_back_b, 0)
     stores[4].start()
+    g_last()
+    stores[3].start()
 
     phase("drain")
     halo_x.wait_send()

time: 79.8 us -> 79.9 us (level)
  no operation moved by 1% of the time
where the time goes in v6:
time: 79.9 us; the launch traced here: 79.8 us
  Pallas kernels  78.9 us (99%)
  between operations  0.81 us (1%)
    pallas_call x1, Pallas kernels, shards(): pl.pallas_call(functools.partial(kernel, (n_seq, n_tp, ch * n_tp)), out_s...  75.4 us
    pallas_call x1, Pallas kernels, shards(): pl.pallas_call(publish, out_shape=[jax.ShapeDtypeStruct(v.shape, v.dtype)...  3.51 us

profile of v6, /device:TPU:1, one launch (start us, length us, event | category | flops | bytes accessed | tf_op | source)
XLA Modules:
  0.0 79.8 jit_solution(15512233744953007521)
XLA Ops:
  0.6 75.4 %mixer.1 = (bf16[320,512]{1,0:T(8,128)(2,1)}, f32[512,640]{1,0:T(8,128)}, f32[512,640]{1,0:T(8,128)}, f32[512,256]{1,0:T(8,128)}, f32[10,512]{1,0:T(8,128)}, /*index=5*/f32[160,640]{1,0:T(8,128)}) custom-call(bf16[512,640]{1,0:T(8,128)(2,1)} %ix_in.1, bf16[512,640]{1,0:T(8,128)(2,1)} %gz_in.1, bf16[512,256]{1,0:T(8,128)(2,1)} %bc_in.1, ...), custom_call_target="tpu_custom_call" | custom-call | tf_op jit(solution)/shard_map/mixer/pallas_call | solution.py:1194
  76.1 3.5 %publish.1 = (f32[512,640]{1,0:T(8,128)}, f32[512,640]{1,0:T(8,128)}, f32[512,256]{1,0:T(8,128)}, f32[160,640]{1,0:T(8,128)}, bf16[320,512]{1,0:T(8,128)(2,1)}, /*index=5*/f32[10,512]{1,0:T(8,128)}) custom-call(f32[512,640]{1,0:T(8,128)} %get-tuple-element.18.refs_0_, f32[512,640]{1,0:T(8,128)} %get-tuple-element.19.refs_1_, ...), custom_call_target="tpu_custom_call" | custom-call | tf_op jit(solution)/shard_map/publish/pallas_call | solution.py:1229
